TPU v7x, 128 devices: a whole 4x4x4 slice. The times are simulated.
128 devices in a mesh: gx: 8 (over x, y_hi), gy: 16 (over y_lo, z, core).
Axes of the slice: x: 4, y: 4 (y_hi: 2, y_lo: 2; y = y_hi * 2 + y_lo), z: 4, core: 2. Of those that a mesh axis runs over, the one named last changes fastest.
Arguments:
- value_field: float32 [4, 48, 96, 1536], P(None, 'gx', 'gy'), may hold values from -16 to 17
- target_mask: int32 [4, 48, 96, 1536], P(None, 'gx', 'gy'), may hold values 0 or 1
- obstacle_mask: int32 [4, 48, 96, 1536], P(None, 'gx', 'gy'), may hold values 0 or 1
- drift_gains: float32 [5], replicated, may hold values from 0.5 to 2
- control_costs: float32 [5], replicated, may hold values from 0.25 to 1
Outputs:
- reach_value: float32 [4, 48, 96, 1536], P(None, 'gx', 'gy')
- time_steps: float32 [3], replicated
All inputs are finite; a program needn't handle non-finite values. No bound on the sum of `target_mask` or of `obstacle_mask` on one device may be relied on, other than what follows from the above.
Results may differ from a plain program's by a relative error of at most 0.0003.
Values sent between devices are 32-bit elements; how exact they have to be, the bound alone decides.
A program may use at most 128 MiB of HBM per device.

v0:
```python
import functools
import math

import jax
import jax.numpy as jnp
from jax import lax
from jax.experimental import pallas as pl
from jax.experimental.pallas import tpu as pltpu
from jax.sharding import PartitionSpec as P

PLANES, N3, N4, GRID, STEPS, NA, NB = 4, 32, 48, 96, 3, 48, 96
SPACING = (2.0 / GRID, 2.0 * math.pi / NA, 2.0 * math.pi / NB, 2.0 / GRID, 2.0 / GRID)
MESH = pl.DeviceIdType.MESH
F32 = jnp.float32
BIG = 3.0e38

ROWS_A, COLS_B, CHUNKS = 12, 6, 6
CELL = PLANES * CHUNKS
LINE = COLS_B * CELL
TOTAL = ROWS_A * LINE
GROUPS = 5
PADDED = GROUPS * 384
PITCH = 52
SLOTS = 14
GHOST = 3
EPS = 0.75e-6


def _add(x, y):
    if x is None:
        return y
    if y is None:
        return x
    return x + y


def _sub(x, y):
    if y is None:
        return x
    if x is None:
        return -y
    return x - y


def _mul(x, y):
    if x is None or y is None:
        return None
    return x * y


def chain(values):
    cells = len(values) - 6
    diffs = [
        None if values[i] is values[i + 1] else values[i + 1] - values[i]
        for i in range(cells + 5)
    ]
    curve, twice, lean, weight_x, weight_y, weight_z = {}, {}, {}, {}, {}, {}
    previous = None

    def curve_at(i):
        if i not in curve:
            curve[i] = _sub(diffs[i + 1], diffs[i])
            twice[i] = _add(curve[i], curve[i])
            square = _mul(curve[i], curve[i])
            lean[i] = (square, _mul(square, 1.5))
        return curve[i]

    def smooth_at(i):
        if i not in weight_x:
            now, last = curve_at(i), curve_at(i - 1)
            cross = _mul(now, last)
            base = _add(lean[i][0], lean[i - 1][0])
            base = EPS if base is None else base + EPS
            middle = _sub(base, _mul(cross, 2.75))
            x = _add(middle, lean[i][1])
            y = _add(middle, lean[i - 1][1])
            z = _add(middle, _mul(cross, 1.5))
            weight_x[i], weight_y[i], weight_z[i] = x * x, y * y, z * z

    def third_at(i):
        return _sub(_add(curve_at(i + 1), curve_at(i - 1)), twice[i])

    thirds = {}
    for face in range(2, cells + 3):
        for i in (face - 1, face, face + 1):
            smooth_at(i)
        one, two, three = weight_x[face - 1], weight_z[face], weight_y[face + 1]
        w_low, w_mid, w_high = two * three, one * three, one * two
        for i in (face - 1, face):
            if i not in thirds:
                thirds[i] = third_at(i)
        low = _mul(thirds[face - 1], w_low)
        high = _mul(thirds[face], w_high)
        base = ((w_low + w_high) + (w_mid + w_mid)) * 1.5
        now, last = curve[face], curve[face - 1]
        scaled = _mul(diffs[face], 6.0)
        left = right = None
        if face < cells + 2:
            top = _add(low, _mul(high, 1.5))
            left = _add(scaled, _add(last, twice[face]))
            if top is not None:
                left = _sub(left, top * pl.reciprocal(base - w_low, approx=True))
        if face > 2:
            top = _add(_mul(low, 1.5), high)
            right = _sub(scaled, _add(now, twice[face - 1]))
            if top is not None:
                right = _add(right, top * pl.reciprocal(base - w_high, approx=True))
            yield previous, right
        previous = left


def kernel(
    value_hbm, target_hbm, obstacle_hbm, gains, costs,
    out_hbm, steps_out,
    val, hn, d_a, d_b, d_p, wn, hi, lo,
    ghost_al, ghost_ah, ghost_bl, ghost_bh,
    tr, ht, d_3, d_4, side_out, side_in,
    stage_own, stage_other, mask_own, mask_other,
    tab_f1, tab_f2, tab_sa, tab_ab, tab_x3, tab_l3, tab_l4,
    ar_src, ar_buf,
    local_sem, swap_s, swap_r, halo_s, halo_r, ar_s, ar_r, out_sem, out_s, out_r,
):
    gx, gy = lax.axis_index("gx"), lax.axis_index("gy")
    half = lax.rem(gx, 2)
    other = 1 - half
    partner = (gx + 1 - 2 * half, gy)
    me = gx * 16 + gy

    def remote(src, dst, send, recv, device):
        return pltpu.make_async_remote_copy(
            src_ref=src, dst_ref=dst, send_sem=send, recv_sem=recv,
            device_id=device, device_id_type=MESH,
        )

    def lanes_of(ref, which):
        return ref.at[:, :, :, pl.ds(pl.multiple_of(which * 768, 128), 768)]

    inputs = (value_hbm, target_hbm, obstacle_hbm)
    others = (stage_other, mask_other.at[0], mask_other.at[1])
    owns = (stage_own, mask_own.at[0], mask_own.at[1])
    swaps = [
        remote(lanes_of(inputs[k], other), others[k], swap_s.at[k], swap_r.at[k], partner)
        for k in range(3)
    ]
    locals_ = [
        pltpu.make_async_copy(lanes_of(inputs[k], half), owns[k], local_sem.at[k])
        for k in range(3)
    ]
    swaps[0].start()
    for k in range(3):
        locals_[k].start()

    lane8 = lax.broadcasted_iota(jnp.int32, (8, 128), 1)
    lane8f = lane8.astype(F32)
    odd = (lane8 & 1) == 1

    def splat(scalar):
        return jnp.full((8, 128), scalar, F32)

    fscale = [splat(12.0 * gains[i]) / splat(costs[i]) for i in range(5)]
    kk = [costs[i] * (1.0 / (288.0 * SPACING[i])) for i in range(5)]
    half_f = half.astype(F32)
    first_a = (lax.div(gx, 2) * ROWS_A).astype(F32)
    first_b = (gy * COLS_B).astype(F32)
    step_a, step_b = 2.0 * math.pi / NA, 2.0 * math.pi / NB
    cell = 2.0 / GRID

    def split_lane(merged):
        third = jnp.floor((merged + 0.5) * (1.0 / N4))
        return third, merged - third * N4

    for block in range(3):
        row = lax.broadcasted_iota(jnp.int32, (8, 128), 0).astype(F32) + 8.0 * block
        plane = jnp.floor((row + 0.5) * (1.0 / CHUNKS))
        merged = (half_f * CHUNKS + row - plane * CHUNKS) * 128.0 + lane8f
        third, fourth = split_lane(merged)
        x0 = (plane - PLANES / 2 + 0.5) * cell
        x3 = (third - N3 / 2 + 0.5) * cell
        x4 = (fourth - N4 / 2 + 0.5) * cell
        tab_f1[pl.ds(8 * block, 8)] = fscale[1] * (x4 - 0.3 * x0)
        tab_f2[pl.ds(8 * block, 8)] = fscale[2] * x3
    for chunk in range(CHUNKS):
        third, _ = split_lane((half_f * CHUNKS + chunk) * 128.0 + lane8f)
        tab_x3[pl.ds(8 * chunk, 8)] = fscale[0] * ((third - N3 / 2 + 0.5) * cell)

    def table_row(i, carry):
        angle = step_a * (splat(first_a) + i.astype(F32))
        tab_sa[pl.ds(pl.multiple_of(8 * i, 8), 8)] = fscale[2] * (0.5 * jnp.sin(angle))
        return carry

    lax.fori_loop(0, ROWS_A, table_row, 0)

    def table_ab(i, carry):
        row = lax.broadcasted_iota(jnp.int32, (8, 128), 0).astype(F32) + 8.0 * i.astype(F32)
        a = jnp.floor((row + 0.5) * (1.0 / COLS_B))
        b = row - a * COLS_B
        tab_ab[pl.ds(pl.multiple_of(8 * i, 8), 8)] = fscale[0] * (
            jnp.cos(step_a * (first_a + a)) - 0.5 * jnp.cos(step_b * (first_b + b))
        )
        return carry

    lax.fori_loop(0, 9, table_ab, 0)

    def table_lane(g, carry):
        spot = lane8f + 128.0 * g.astype(F32)
        pair = jnp.floor((spot + 0.5) * 0.125)
        plane = jnp.floor((spot - pair * 8.0 + 0.5) * 0.5)
        a = jnp.floor((pair + 0.5) * (1.0 / COLS_B))
        b = pair - a * COLS_B
        sin_b = jnp.sin(step_b * (first_b + b))
        x0 = (plane - PLANES / 2 + 0.5) * cell
        keep = spot < 576.0
        where = pl.ds(pl.multiple_of(8 * g, 8), 8)
        tab_l3[where] = jnp.where(keep, fscale[3] * (sin_b - x0), 0.0)
        tab_l4[where] = jnp.where(keep, fscale[4] * (jnp.cos(step_a * (first_a + a)) * sin_b), 0.0)
        return carry

    lax.fori_loop(0, GROUPS, table_lane, 0)
    for i in range(TOTAL // 8, PADDED // 8):
        val[pl.ds(8 * i, 8)] = jnp.zeros((8, 128), F32)

    def spread(stage, target_rows, convert=None):
        def body(a, carry):
            for p in range(PLANES):
                for c in range(CHUNKS):
                    tile = stage[p, a, :, pl.ds(128 * c, 128)]
                    start = (target_rows + a) * LINE + p * CHUNKS + c
                    if convert is None:
                        val[pl.ds(start, COLS_B, stride=CELL)] = tile
                    else:
                        ref, bound, free = convert
                        ref[pl.ds(start, COLS_B, stride=CELL)] = jnp.where(tile == 1, bound, free)
            return carry

        lax.fori_loop(0, 6, body, 0)

    locals_[0].wait()
    spread(stage_own, half * 6)
    swaps[0].wait_recv()
    spread(stage_other, other * 6)

    row_before = (lax.rem(gx + 6, 8), gy)
    row_after = (lax.rem(gx + 2, 8), gy)
    col_before = (gx, lax.rem(gy + 15, 16))
    col_after = (gx, lax.rem(gy + 1, 16))

    def whole(ref, k):
        return remote(ref, ref, halo_s.at[k], halo_r.at[k], partner)

    halo_refs = (ghost_al, ghost_ah, ghost_bl, ghost_bh, side_in)

    def start_side():
        remote(side_out, side_in, halo_s.at[4], halo_r.at[4], partner).start()

    def start_halos():
        for a in range(ROWS_A):
            remote(
                val.at[pl.ds(a * LINE + 72, 72)], ghost_bl.at[pl.ds(a * 72, 72)],
                halo_s.at[2], halo_r.at[2], col_after,
            ).start()
            remote(
                val.at[pl.ds(a * LINE, 72)], ghost_bh.at[pl.ds(a * 72, 72)],
                halo_s.at[3], halo_r.at[3], col_before,
            ).start()
        remote(
            val.at[pl.ds((ROWS_A - 3) * LINE, 3 * LINE)], ghost_al,
            halo_s.at[0], halo_r.at[0], row_after,
        ).start()
        remote(
            val.at[pl.ds(0, 3 * LINE)], ghost_ah,
            halo_s.at[1], halo_r.at[1], row_before,
        ).start()

    def tr_row(g, slot):
        return g * (SLOTS * PITCH) + slot * PITCH

    def to_transposed():
        def body(g, carry):
            for r in range(3):
                block = val[pl.ds(g * 384 + r, 128, stride=3)].T
                for k in range(16):
                    merged = r * 128 + 8 * k
                    row = tr_row(g, GHOST + merged // N4) + merged % N4
                    tr[pl.ds(row, 8)] = block[8 * k:8 * k + 8]
            return carry

        lax.fori_loop(0, GROUPS, body, 0)

    is_low = half == 0
    turn = jnp.where(is_low, 127, 1)
    mine = jnp.where(is_low, lane8 & 1, 1 - (lane8 & 1)) == 0
    send_slot = jnp.where(is_low, GHOST + 5, GHOST)

    def pack_side():
        def body(k, carry):
            for s in range(3):
                for q in range(6):
                    one = tr[pl.ds(tr_row(2 * k, send_slot + s) + 8 * q, 8)]
                    two = tr[pl.ds(tr_row(jnp.minimum(2 * k + 1, 4), send_slot + s) + 8 * q, 8)]
                    side_out[pl.ds(k * 144 + s * 48 + 8 * q, 8)] = jnp.where(
                        mine, pltpu.roll(one, turn, 1), two
                    )
            return carry

        lax.fori_loop(0, 3, body, 0)

    def merge_side():
        def body(g, carry):
            pack = lax.div(g, 2)
            second = lax.rem(g, 2) == 1
            back = jnp.where(is_low, 1, 127)
            for s in range(3):
                for q in range(6):
                    at = 8 * q
                    got = side_in[pl.ds(pack * 144 + s * 48 + at, 8)]
                    got = jnp.where(second, pltpu.roll(got, back, 1), got)
                    top = tr[pl.ds(tr_row(g, GHOST + 7) + at, 8)]
                    bottom = tr[pl.ds(tr_row(g, GHOST) + at, 8)]
                    up = pltpu.roll(tr[pl.ds(tr_row(g, GHOST + s) + at, 8)], 127, 1)
                    down = pltpu.roll(tr[pl.ds(tr_row(g, GHOST + 5 + s) + at, 8)], 1, 1)
                    tr[pl.ds(tr_row(g, GHOST + 8 + s) + at, 8)] = jnp.where(
                        odd, jnp.where(is_low, got, top), up
                    )
                    tr[pl.ds(tr_row(g, s) + at, 8)] = jnp.where(
                        odd, down, jnp.where(is_low, bottom, got)
                    )
            return carry

        lax.fori_loop(0, GROUPS, body, 0)

    def cell_out(left, right, flow, square, factor, peak):
        total = left + right
        gap = right - left
        rest = flow - total
        peak = jnp.maximum(peak, jnp.abs(rest) + jnp.abs(gap))
        return gap, (square - rest * rest) * factor, peak

    zero = jnp.zeros((8, 128), F32)

    def along_planes():
        def body(n, peak):
            q, c = lax.div(n, CHUNKS), lax.rem(n, CHUNKS)
            start = q * (8 * CELL) + c
            rows = [pl.ds(start + p * CHUNKS, 8, stride=CELL) for p in range(PLANES)]
            got = [val[rows[p]] for p in range(PLANES)]
            flow = tab_ab[pl.ds(pl.multiple_of(8 * q, 8), 8)] + tab_x3[
                pl.ds(pl.multiple_of(8 * c, 8), 8)
            ]
            square = flow * flow
            line = [got[0]] * 3 + got + [got[3]] * 3
            for p, (left, right) in enumerate(chain(line)):
                left = zero if left is None else left
                right = zero if right is None else right
                gap, part, peak = cell_out(left, right, flow, square, kk[0], peak)
                d_p[rows[p]] = gap
                hn[rows[p]] = part
            return peak

        return lax.fori_loop(0, 9 * CHUNKS, body, zero)

    def along_rows():
        def body(n, peak):
            at = pl.multiple_of(8 * n, 8)
            line = (
                [ghost_al[pl.ds(i * LINE + at, 8)] for i in range(3)]
                + [val[pl.ds(a * LINE + at, 8)] for a in range(ROWS_A)]
                + [ghost_ah[pl.ds(i * LINE + at, 8)] for i in range(3)]
            )
            flow = tab_f1[pl.ds(pl.multiple_of(8 * lax.rem(n, 3), 8), 8)]
            square = flow * flow
            for a, (left, right) in enumerate(chain(line)):
                gap, part, peak = cell_out(left, right, flow, square, kk[1], peak)
                where = pl.ds(a * LINE + at, 8)
                d_a[where] = gap
                hn[where] += part
            return peak

        return lax.fori_loop(0, LINE // 8, body, zero)

    def along_cols():
        def body(n, peak):
            a, j = lax.div(n, 3), lax.rem(n, 3)
            ghost = pl.multiple_of(a * 72 + 8 * j, 8)
            at = pl.multiple_of(a * LINE + 8 * j, 8)
            line = (
                [ghost_bl[pl.ds(ghost + i * CELL, 8)] for i in range(3)]
                + [val[pl.ds(at + b * CELL, 8)] for b in range(COLS_B)]
                + [ghost_bh[pl.ds(ghost + i * CELL, 8)] for i in range(3)]
            )
            flow = tab_f2[pl.ds(pl.multiple_of(8 * j, 8), 8)] + tab_sa[
                pl.ds(pl.multiple_of(8 * a, 8), 8)
            ]
            square = flow * flow
            for b, (left, right) in enumerate(chain(line)):
                gap, part, peak = cell_out(left, right, flow, square, kk[2], peak)
                where = pl.ds(at + b * CELL, 8)
                d_b[where] = gap
                hn[where] += part
            return peak

        return lax.fori_loop(0, 3 * ROWS_A, body, zero)

    def along_third():
        def body(n, peak):
            g, q = lax.div(n, 6), lax.rem(n, 6)
            line = [tr[pl.ds(tr_row(g, s) + 8 * q, 8)] for s in range(SLOTS)]
            flow = tab_l3[pl.ds(pl.multiple_of(8 * g, 8), 8)]
            square = flow * flow
            for s, (left, right) in enumerate(chain(line)):
                gap, part, peak = cell_out(left, right, flow, square, kk[3], peak)
                where = pl.ds((g * 8 + s) * PITCH + 8 * q, 8)
                d_3[where] = gap
                ht[where] += part
            return peak

        return lax.fori_loop(0, GROUPS * 6, body, zero)

    slope4 = fscale[4] * cell

    def along_fourth():
        def body(n, peak):
            g, seg = lax.div(n, 4), lax.rem(n, 4)
            first = seg * 12
            line = []
            for i in range(-3, 15):
                at = first + i
                if i < 0:
                    at = jnp.maximum(at, 0)
                if i > 11:
                    at = jnp.minimum(at, N4 - 1)
                line.append(tr[pl.ds(tr_row(g, GHOST) + at, 8, stride=PITCH)])
            table = tab_l4[pl.ds(pl.multiple_of(8 * g, 8), 8)]
            base = table - slope4 * (first.astype(F32) - (N4 / 2 - 0.5))
            for i, (left, right) in enumerate(chain(line)):
                flow = base - slope4 * float(i)
                gap, part, peak = cell_out(left, right, flow, flow * flow, kk[4], peak)
                where = pl.ds(g * 8 * PITCH + first + i, 8, stride=PITCH)
                d_4[where] = gap
                ht[where] = part
            return peak

        return lax.fori_loop(0, GROUPS * 4, body, zero)

    def speeds(step, peaks):
        row = jnp.zeros((1, 128), F32)
        lane = lax.broadcasted_iota(jnp.int32, (1, 128), 1)
        for i, peak in enumerate(peaks):
            row = jnp.where(lane == i, jnp.max(peak), row)
        ar_src[step] = row
        ar_buf[step, me] = row

        def send(k, carry):
            to = lax.rem(me + k, 128)
            remote(
                ar_src.at[step], ar_buf.at[step, me], ar_s.at[step], ar_r.at[step],
                (lax.div(to, 16), lax.rem(to, 16)),
            ).start()
            return carry

        lax.fori_loop(1, 128, send, 0)

    def all_speeds(step):
        every = ar_buf.at[step, pl.ds(0, 127)]
        whole_row = remote(every, every, ar_s.at[step], ar_r.at[step], partner)
        whole_row.wait_recv()
        best = jnp.max(ar_buf[step], axis=0)
        whole_row.wait_send()
        speed = []
        for i in range(5):
            lane_max = jnp.broadcast_to(best[:, i:i + 1], (8, 128))
            speed.append(lane_max * (costs[i] * (1.0 / 12.0)))
        summed = zero
        for i in range(5):
            summed = summed + speed[i] / SPACING[i]
        time_step = 0.5 / (summed + 1e-6)
        steps_out[step] = time_step[0, 0]
        return time_step, [
            time_step * speed[i] * (1.0 / (12.0 * SPACING[i])) for i in range(5)
        ]

    def from_transposed(dt, coef):
        def body(g, carry):
            for r in range(3):
                parts = []
                for k in range(16):
                    merged = r * 128 + 8 * k
                    row = (g * 8 + merged // N4) * PITCH + merged % N4
                    where = pl.ds(row, 8)
                    parts.append(coef[3] * d_3[where] + coef[4] * d_4[where] - dt * ht[where])
                block = jnp.concatenate(parts, axis=0).T
                wn[pl.ds(g * 384 + r, 128, stride=3)] = block
            return carry

        lax.fori_loop(0, GROUPS, body, 0)

    def new_row(at, dt, coef):
        where = pl.ds(at, 8)
        moved = val[where] + wn[where] - dt * hn[where]
        moved = moved + coef[0] * d_p[where] + coef[1] * d_a[where] + coef[2] * d_b[where]
        return jnp.maximum(jnp.minimum(moved, hi[where]), lo[where])

    def update(dt, coef):
        def body(n, carry):
            for i in range(4):
                at = pl.multiple_of(32 * n + 8 * i, 8)
                val[pl.ds(at, 8)] = new_row(at, dt, coef)
            return carry

        lax.fori_loop(0, TOTAL // 32, body, 0)

    def out_copy(stage, a, which):
        return stage.at[:, a], out_hbm.at[:, a, :, pl.ds(pl.multiple_of(which * 768, 128), 768)]

    def last_update(dt, coef):
        def rows(first, stage, launch):
            def body(a, carry):
                for i in range(LINE // 8):
                    at = pl.multiple_of((first + a) * LINE + 8 * i, 8)
                    val[pl.ds(at, 8)] = new_row(at, dt, coef)
                for p in range(PLANES):
                    for c in range(CHUNKS):
                        start = (first + a) * LINE + p * CHUNKS + c
                        stage[p, a, :, pl.ds(128 * c, 128)] = val[
                            pl.ds(start, COLS_B, stride=CELL)
                        ]
                launch(a)
                return carry

            lax.fori_loop(0, 6, body, 0)

        def far(a):
            src, dst = out_copy(stage_other, a, half)
            remote(src, dst, out_s, out_r, partner).start()

        def near(a):
            src, dst = out_copy(stage_own, a, half)
            pltpu.make_async_copy(src, dst, out_sem).start()

        rows(other * 6, stage_other, far)
        rows(half * 6, stage_own, near)
        done = pltpu.make_async_copy(stage_own, lanes_of(out_hbm, half), out_sem)
        done.wait()
        sent = remote(stage_other, lanes_of(out_hbm, other), out_s, out_r, partner)
        sent.wait_send()
        sent.wait_recv()

    for step in range(STEPS):
        to_transposed()
        pack_side()
        start_side()
        start_halos()
        if step == 0:
            swaps[1].start()
            swaps[2].start()
        peak_p = along_planes()
        peak_4 = along_fourth()
        whole(side_in, 4).wait_recv()
        merge_side()
        peak_3 = along_third()
        whole(ghost_bl, 2).wait_recv()
        whole(ghost_bh, 3).wait_recv()
        peak_b = along_cols()
        whole(ghost_al, 0).wait_recv()
        whole(ghost_ah, 1).wait_recv()
        peak_a = along_rows()
        speeds(step, [peak_p, peak_a, peak_b, peak_3, peak_4])
        for k, ref in enumerate(halo_refs):
            whole(ref, k).wait_send()
        if step == 0:
            for k in (1, 2):
                locals_[k].wait()
            spread(owns[1], half * 6, (hi, -0.5, BIG))
            spread(owns[2], half * 6, (lo, 0.5, -BIG))
            for k in (1, 2):
                swaps[k].wait_recv()
            spread(others[1], other * 6, (hi, -0.5, BIG))
            spread(others[2], other * 6, (lo, 0.5, -BIG))
            for k in range(3):
                swaps[k].wait_send()
        dt, coef = all_speeds(step)
        from_transposed(dt, coef)
        if step < STEPS - 1:
            update(dt, coef)
        else:
            last_update(dt, coef)


def solution(mesh):
    def rows(n):
        return pltpu.VMEM((n, 128), F32)

    dma = pltpu.SemaphoreType.DMA
    stage = (PLANES, 6, 6, 768)
    trans = GROUPS * 8 * PITCH
    scratch = [
        rows(PADDED), rows(TOTAL), rows(TOTAL), rows(TOTAL), rows(TOTAL), rows(PADDED),
        rows(TOTAL), rows(TOTAL),
        rows(3 * LINE), rows(3 * LINE), rows(ROWS_A * 72), rows(ROWS_A * 72),
        rows(GROUPS * SLOTS * PITCH), rows(trans), rows(trans), rows(trans),
        rows(432), rows(432),
        pltpu.VMEM(stage, F32), pltpu.VMEM(stage, F32),
        pltpu.VMEM((2,) + stage, jnp.int32), pltpu.VMEM((2,) + stage, jnp.int32),
        rows(24), rows(24), rows(8 * ROWS_A), rows(72), rows(8 * CHUNKS),
        rows(8 * GROUPS), rows(8 * GROUPS),
        pltpu.VMEM((STEPS, 1, 128), F32), pltpu.VMEM((STEPS, 128, 1, 128), F32),
        dma((3,)), dma((3,)), dma((3,)), dma((5,)), dma((5,)), dma((STEPS,)), dma((STEPS,)),
        dma(()), dma(()), dma(()),
    ]

    def body(value_field, target_mask, obstacle_mask, drift_gains, control_costs):
        anywhere = pl.BlockSpec(memory_space=pl.ANY)
        scalars = pl.BlockSpec(memory_space=pltpu.SMEM)
        return pl.pallas_call(
            kernel,
            out_shape=(
                jax.ShapeDtypeStruct(value_field.shape, F32),
                jax.ShapeDtypeStruct((STEPS,), F32),
            ),
            in_specs=[anywhere, anywhere, anywhere, scalars, scalars],
            out_specs=(anywhere, scalars),
            scratch_shapes=scratch,
            compiler_params=pltpu.CompilerParams(
                has_side_effects=True, vmem_limit_bytes=56 * 2**20
            ),
        )(value_field, target_mask, obstacle_mask, drift_gains, control_costs)

    grid = P(None, "gx", "gy", None)
    return jax.shard_map(
        body, mesh=mesh, in_specs=(grid, grid, grid, P(), P()), out_specs=(grid, P()),
        check_vma=False,
    )
```

profile of v0, /device:TPU:1, one launch (start us, length us, event | category | flops | bytes accessed | tf_op | source)
XLA Modules:
  0.0 146.0 jit_solution(16208136785616199170)
XLA Ops:
  0.6 0.0 copy-start
  0.6 2.6 %copy.7.value_hbm = f32[4,6,6,1536]{3,2,1,0:T(8,128)} copy(f32[4,6,6,1536]{3,0,2,1:T(4,128)} %param.5) | data formatting | bytes 1769472 | tf_op args[0]
  3.2 0.0 copy-done
  3.2 0.0 copy-start.1
  3.2 1.3 copy.8.target_hbm
  4.5 0.0 copy-done.1
  4.5 1.3 copy.9.obstacle_hbm
  5.8 136.9 %shard_map.68 = (f32[4,6,6,1536]{3,2,1,0:T(8,128)}, f32[3]{0:T(128)}) custom-call(f32[4,6,6,1536]{3,2,1,0:T(8,128)} %copy.7.value_hbm, s32[4,6,6,1536]{3,2,1,0:T(8,128)} %copy.8.target_hbm, s32[4,6,6,1536]{3,2,1,0:T(8,128)} %copy.9.obstacle_hbm, f32[5]{0:T(128)} %gains.1, f32[5]{0:T(128)} %costs.1), custom_call_target="tpu_custom_call" | custom-call | tf_op jit(solution)/shard_map/pallas_call | solution.py:613
  142.7 0.0 copy-start.2
  142.7 2.8 %copy.10 = f32[4,6,6,1536]{3,0,2,1:T(4,128)} copy(f32[4,6,6,1536]{3,2,1,0:T(8,128)} %get-tuple-element.2) | data formatting | bytes 1769472 | tf_op jit(solution)/shard_map/pallas_call | solution.py:613
  145.5 0.0 copy-done.2
  145.5 0.5 copy.12
Async XLA Ops:
  0.6 2.6 %copy-start = (s32[4,6,6,1536]{3,0,2,1:T(4,128)S(1)}, s32[4,6,6,1536]{3,0,2,1:T(4,128)}, u32[]{:S(2)}) copy-start(s32[4,6,6,1536]{3,0,2,1:T(4,128)} %param.6) | copy-start | bytes 2654212
  3.2 1.3 copy-start.1
  142.7 2.8 %copy-start.2 = (f32[3]{0:T(128)S(1)}, f32[3]{0:T(128)}, u32[]{:S(2)}) copy-start(f32[3]{0:T(128)} %get-tuple-element.7) | copy-start | bytes 40
where the time goes:
time: 146 us
  Pallas kernels  137 us (94%)
  local copies, waits for them, and re-layouts  8.47 us (6%)
    pallas_call x1, Pallas kernels, body(): pl.pallas_call(kernel, out_shape=(jax.ShapeDtypeStruct(value_field.shape,...  137 us
    unnamed x10, local copies, waits for them, and re-layouts  5.72 us

commit v1 on v0

--- a/solution.py
+++ b/solution.py
@@ -19,11 +19,22 @@
 LINE = COLS_B * CELL
 TOTAL = ROWS_A * LINE
 GROUPS = 5
-PADDED = GROUPS * 384
 PITCH = 52
 SLOTS = 14
 GHOST = 3
 EPS = 0.75e-6
+
+
+def _hops(offset):
+    dx, dy = offset
+    ring = lambda n: min(n, 4 - n)
+    return ring(dx // 2) + 2 * (dx % 2) + ring(dy // 2 % 4) + dy // 8
+
+
+FAR_FIRST = sorted(
+    [(dx, dy) for dx in range(8) for dy in range(16) if dx or dy], key=_hops, reverse=True
+)
+ROUNDS = (((0, 1), (0, 15)), ((0, 2), (0, 14)), ((0, 4), (0, 12)), ((2, 0), (6, 0)), ((4, 0),))
 
 
 def _add(x, y):
@@ -115,10 +126,10 @@
     val, hn, d_a, d_b, d_p, wn, hi, lo,
     ghost_al, ghost_ah, ghost_bl, ghost_bh,
     tr, ht, d_3, d_4, side_out, side_in,
-    stage_own, stage_other, mask_own, mask_other,
+    mask_t, mask_o,
     tab_f1, tab_f2, tab_sa, tab_ab, tab_x3, tab_l3, tab_l4,
     ar_src, ar_buf,
-    local_sem, swap_s, swap_r, halo_s, halo_r, ar_s, ar_r, out_sem, out_s, out_r,
+    met, local_sem, swap_s, swap_r, halo_s, halo_r, ar_s, ar_r, out_sem, out_s, out_r,
 ):
     gx, gy = lax.axis_index("gx"), lax.axis_index("gy")
     half = lax.rem(gx, 2)
@@ -132,23 +143,40 @@
             device_id=device, device_id_type=MESH,
         )
 
-    def lanes_of(ref, which):
-        return ref.at[:, :, :, pl.ds(pl.multiple_of(which * 768, 128), 768)]
+    row_before = (lax.rem(gx + 6, 8), gy)
+    row_after = (lax.rem(gx + 2, 8), gy)
+    col_before = (gx, lax.rem(gy + 15, 16))
+    col_after = (gx, lax.rem(gy + 1, 16))
+    barrier = pltpu.get_barrier_semaphore()
+    for device in (partner, col_before, col_after, row_before, row_after):
+        pl.semaphore_signal(barrier, inc=1, device_id=device, device_id_type=MESH)
+
+    def part_of(ref, which):
+        return ref.at[:, pl.ds(pl.multiple_of(which * CELL, 8), CELL)]
 
     inputs = (value_hbm, target_hbm, obstacle_hbm)
-    others = (stage_other, mask_other.at[0], mask_other.at[1])
-    owns = (stage_own, mask_own.at[0], mask_own.at[1])
+    places = (val, mask_t, mask_o)
+
+    def cells_of(ref, first, count):
+        return ref.reshape(TOTAL // CELL, CELL, 128).at[pl.ds(first, count)]
+
     swaps = [
-        remote(lanes_of(inputs[k], other), others[k], swap_s.at[k], swap_r.at[k], partner)
+        remote(
+            part_of(inputs[k], other), cells_of(places[k], half * 36, 36),
+            swap_s.at[k], swap_r.at[k], partner,
+        )
         for k in range(3)
     ]
     locals_ = [
-        pltpu.make_async_copy(lanes_of(inputs[k], half), owns[k], local_sem.at[k])
+        pltpu.make_async_copy(
+            part_of(inputs[k], half), cells_of(places[k], half * 36, 36), local_sem.at[k]
+        )
         for k in range(3)
     ]
-    swaps[0].start()
     for k in range(3):
         locals_[k].start()
+    pl.semaphore_wait(barrier, 5)
+    swaps[0].start()
 
     lane8 = lax.broadcasted_iota(jnp.int32, (8, 128), 1)
     lane8f = lane8.astype(F32)
@@ -171,8 +199,9 @@
 
     for block in range(3):
         row = lax.broadcasted_iota(jnp.int32, (8, 128), 0).astype(F32) + 8.0 * block
-        plane = jnp.floor((row + 0.5) * (1.0 / CHUNKS))
-        merged = (half_f * CHUNKS + row - plane * CHUNKS) * 128.0 + lane8f
+        chunk = jnp.floor((row + 0.5) * (1.0 / PLANES))
+        plane = row - chunk * PLANES
+        merged = (half_f * CHUNKS + chunk) * 128.0 + lane8f
         third, fourth = split_lane(merged)
         x0 = (plane - PLANES / 2 + 0.5) * cell
         x3 = (third - N3 / 2 + 0.5) * cell
@@ -202,47 +231,23 @@
     lax.fori_loop(0, 9, table_ab, 0)
 
     def table_lane(g, carry):
-        spot = lane8f + 128.0 * g.astype(F32)
-        pair = jnp.floor((spot + 0.5) * 0.125)
-        plane = jnp.floor((spot - pair * 8.0 + 0.5) * 0.5)
+        last = g == GROUPS - 1
+        piece = jnp.floor((lane8f + 0.5) * 0.0625)
+        plane = jnp.where(last, piece, g.astype(F32))
+        spot = jnp.where(last, 128.0 + lane8f - 16.0 * piece, lane8f)
+        pair = jnp.floor((spot + 0.5) * 0.5)
         a = jnp.floor((pair + 0.5) * (1.0 / COLS_B))
         b = pair - a * COLS_B
         sin_b = jnp.sin(step_b * (first_b + b))
         x0 = (plane - PLANES / 2 + 0.5) * cell
-        keep = spot < 576.0
+        keep = plane < 4.0
         where = pl.ds(pl.multiple_of(8 * g, 8), 8)
         tab_l3[where] = jnp.where(keep, fscale[3] * (sin_b - x0), 0.0)
         tab_l4[where] = jnp.where(keep, fscale[4] * (jnp.cos(step_a * (first_a + a)) * sin_b), 0.0)
         return carry
 
     lax.fori_loop(0, GROUPS, table_lane, 0)
-    for i in range(TOTAL // 8, PADDED // 8):
-        val[pl.ds(8 * i, 8)] = jnp.zeros((8, 128), F32)
-
-    def spread(stage, target_rows, convert=None):
-        def body(a, carry):
-            for p in range(PLANES):
-                for c in range(CHUNKS):
-                    tile = stage[p, a, :, pl.ds(128 * c, 128)]
-                    start = (target_rows + a) * LINE + p * CHUNKS + c
-                    if convert is None:
-                        val[pl.ds(start, COLS_B, stride=CELL)] = tile
-                    else:
-                        ref, bound, free = convert
-                        ref[pl.ds(start, COLS_B, stride=CELL)] = jnp.where(tile == 1, bound, free)
-            return carry
-
-        lax.fori_loop(0, 6, body, 0)
-
     locals_[0].wait()
-    spread(stage_own, half * 6)
-    swaps[0].wait_recv()
-    spread(stage_other, other * 6)
-
-    row_before = (lax.rem(gx + 6, 8), gy)
-    row_after = (lax.rem(gx + 2, 8), gy)
-    col_before = (gx, lax.rem(gy + 15, 16))
-    col_after = (gx, lax.rem(gy + 1, 16))
 
     def whole(ref, k):
         return remote(ref, ref, halo_s.at[k], halo_r.at[k], partner)
@@ -252,39 +257,49 @@
     def start_side():
         remote(side_out, side_in, halo_s.at[4], halo_r.at[4], partner).start()
 
-    def start_halos():
-        for a in range(ROWS_A):
-            remote(
-                val.at[pl.ds(a * LINE + 72, 72)], ghost_bl.at[pl.ds(a * 72, 72)],
-                halo_s.at[2], halo_r.at[2], col_after,
-            ).start()
-            remote(
-                val.at[pl.ds(a * LINE, 72)], ghost_bh.at[pl.ds(a * 72, 72)],
-                halo_s.at[3], halo_r.at[3], col_before,
-            ).start()
+    def start_cols(a):
+        at = pl.multiple_of(a * LINE, 8)
+        to = pl.ds(pl.multiple_of(a * 72, 8), 72)
+        remote(
+            val.at[pl.ds(at + 72, 72)], ghost_bl.at[to], halo_s.at[2], halo_r.at[2], col_after
+        ).start()
+        remote(
+            val.at[pl.ds(at, 72)], ghost_bh.at[to], halo_s.at[3], halo_r.at[3], col_before
+        ).start()
+
+    def start_high():
         remote(
             val.at[pl.ds((ROWS_A - 3) * LINE, 3 * LINE)], ghost_al,
             halo_s.at[0], halo_r.at[0], row_after,
         ).start()
+
+    def start_low():
         remote(
-            val.at[pl.ds(0, 3 * LINE)], ghost_ah,
-            halo_s.at[1], halo_r.at[1], row_before,
+            val.at[pl.ds(0, 3 * LINE)], ghost_ah, halo_s.at[1], halo_r.at[1], row_before
         ).start()
 
     def tr_row(g, slot):
         return g * (SLOTS * PITCH) + slot * PITCH
 
     def to_transposed():
+        def put(g, r, block):
+            for k in range(16):
+                merged = r * 128 + 8 * k
+                row = tr_row(g, GHOST + merged // N4) + merged % N4
+                tr[pl.ds(row, 8)] = block[8 * k:8 * k + 8]
+
         def body(g, carry):
             for r in range(3):
-                block = val[pl.ds(g * 384 + r, 128, stride=3)].T
-                for k in range(16):
-                    merged = r * 128 + 8 * k
-                    row = tr_row(g, GHOST + merged // N4) + merged % N4
-                    tr[pl.ds(row, 8)] = block[8 * k:8 * k + 8]
+                put(g, r, val[pl.ds(r * PLANES + g, 128, stride=12)].T)
             return carry
 
-        lax.fori_loop(0, GROUPS, body, 0)
+        lax.fori_loop(0, GROUPS - 1, body, 0)
+        for r in range(3):
+            parts = [
+                val[pl.ds(1536 + r * PLANES + p, 16, stride=12)] for p in range(PLANES)
+            ]
+            parts.append(jnp.zeros((64, 128), F32))
+            put(GROUPS - 1, r, jnp.concatenate(parts, axis=0).T)
 
     is_low = half == 0
     turn = jnp.where(is_low, 127, 1)
@@ -337,11 +352,12 @@
 
     zero = jnp.zeros((8, 128), F32)
 
-    def along_planes():
+    def along_planes(first, end, peak):
         def body(n, peak):
-            q, c = lax.div(n, CHUNKS), lax.rem(n, CHUNKS)
-            start = q * (8 * CELL) + c
-            rows = [pl.ds(start + p * CHUNKS, 8, stride=CELL) for p in range(PLANES)]
+            i, c = lax.div(n, CHUNKS), lax.rem(n, CHUNKS)
+            q = jnp.where(i < 4, half * 5 + i, jnp.where(i == 4, 4, other * 5 + i - 5))
+            start = q * (8 * CELL) + c * PLANES
+            rows = [pl.ds(start + p, 8, stride=CELL) for p in range(PLANES)]
             got = [val[rows[p]] for p in range(PLANES)]
             flow = tab_ab[pl.ds(pl.multiple_of(8 * q, 8), 8)] + tab_x3[
                 pl.ds(pl.multiple_of(8 * c, 8), 8)
@@ -356,7 +372,7 @@
                 hn[rows[p]] = part
             return peak
 
-        return lax.fori_loop(0, 9 * CHUNKS, body, zero)
+        return lax.fori_loop(first * CHUNKS, end * CHUNKS, body, peak)
 
     def along_rows():
         def body(n, peak):
@@ -441,6 +457,17 @@
 
         return lax.fori_loop(0, GROUPS * 4, body, zero)
 
+    def greet(k):
+        if k < len(ROUNDS):
+            devices = [(lax.rem(gx + dx, 8), lax.rem(gy + dy, 16)) for dx, dy in ROUNDS[k]]
+        else:
+            devices = [partner]
+        for device in devices:
+            pl.semaphore_signal(met.at[k], inc=1, device_id=device, device_id_type=MESH)
+
+    def met_all(k):
+        pl.semaphore_wait(met.at[k], len(ROUNDS[k]) if k < len(ROUNDS) else 1)
+
     def speeds(step, peaks):
         row = jnp.zeros((1, 128), F32)
         lane = lax.broadcasted_iota(jnp.int32, (1, 128), 1)
@@ -449,15 +476,11 @@
         ar_src[step] = row
         ar_buf[step, me] = row
 
-        def send(k, carry):
-            to = lax.rem(me + k, 128)
+        for dx, dy in FAR_FIRST:
             remote(
                 ar_src.at[step], ar_buf.at[step, me], ar_s.at[step], ar_r.at[step],
-                (lax.div(to, 16), lax.rem(to, 16)),
+                (lax.rem(gx + dx, 8), lax.rem(gy + dy, 16)),
             ).start()
-            return carry
-
-        lax.fori_loop(1, 128, send, 0)
 
     def all_speeds(step):
         every = ar_buf.at[step, pl.ds(0, 127)]
@@ -479,130 +502,197 @@
         ]
 
     def from_transposed(dt, coef):
+        def take(g, r):
+            parts = []
+            for k in range(16):
+                merged = r * 128 + 8 * k
+                row = (g * 8 + merged // N4) * PITCH + merged % N4
+                where = pl.ds(row, 8)
+                parts.append(coef[3] * d_3[where] + coef[4] * d_4[where] - dt * ht[where])
+            return jnp.concatenate(parts, axis=0).T
+
         def body(g, carry):
             for r in range(3):
-                parts = []
-                for k in range(16):
-                    merged = r * 128 + 8 * k
-                    row = (g * 8 + merged // N4) * PITCH + merged % N4
-                    where = pl.ds(row, 8)
-                    parts.append(coef[3] * d_3[where] + coef[4] * d_4[where] - dt * ht[where])
-                block = jnp.concatenate(parts, axis=0).T
-                wn[pl.ds(g * 384 + r, 128, stride=3)] = block
+                wn[pl.ds(r * PLANES + g, 128, stride=12)] = take(g, r)
             return carry
 
-        lax.fori_loop(0, GROUPS, body, 0)
-
-    def new_row(at, dt, coef):
-        where = pl.ds(at, 8)
-        moved = val[where] + wn[where] - dt * hn[where]
-        moved = moved + coef[0] * d_p[where] + coef[1] * d_a[where] + coef[2] * d_b[where]
-        return jnp.maximum(jnp.minimum(moved, hi[where]), lo[where])
+        lax.fori_loop(0, GROUPS - 1, body, 0)
+        for r in range(3):
+            block = take(GROUPS - 1, r)
+            for p in range(PLANES):
+                wn[pl.ds(1536 + r * PLANES + p, 16, stride=12)] = block[16 * p:16 * p + 16]
+
+    def new_line(a, dt, coef):
+        for i in range(LINE // 8):
+            where = pl.ds(pl.multiple_of(a * LINE + 8 * i, 8), 8)
+            moved = val[where] + wn[where] - dt * hn[where]
+            moved = moved + coef[0] * d_p[where] + coef[1] * d_a[where] + coef[2] * d_b[where]
+            val[where] = jnp.maximum(jnp.minimum(moved, hi[where]), lo[where])
 
     def update(dt, coef):
+        def line_of(n):
+            return jnp.where(n < 6, jnp.where(n < 3, n, n + 6), n - 3)
+
         def body(n, carry):
-            for i in range(4):
-                at = pl.multiple_of(32 * n + 8 * i, 8)
-                val[pl.ds(at, 8)] = new_row(at, dt, coef)
+            new_line(line_of(n), dt, coef)
+
+            @pl.when(n > 0)
+            def _():
+                start_cols(line_of(n - 1))
+
+            @pl.when(n == 3)
+            def _():
+                start_low()
+
+            @pl.when(n == 6)
+            def _():
+                start_high()
+
             return carry
 
-        lax.fori_loop(0, TOTAL // 32, body, 0)
-
-    def out_copy(stage, a, which):
-        return stage.at[:, a], out_hbm.at[:, a, :, pl.ds(pl.multiple_of(which * 768, 128), 768)]
+        lax.fori_loop(0, ROWS_A, body, 0)
+        start_cols(8)
 
     def last_update(dt, coef):
-        def rows(first, stage, launch):
-            def body(a, carry):
-                for i in range(LINE // 8):
-                    at = pl.multiple_of((first + a) * LINE + 8 * i, 8)
-                    val[pl.ds(at, 8)] = new_row(at, dt, coef)
-                for p in range(PLANES):
-                    for c in range(CHUNKS):
-                        start = (first + a) * LINE + p * CHUNKS + c
-                        stage[p, a, :, pl.ds(128 * c, 128)] = val[
-                            pl.ds(start, COLS_B, stride=CELL)
-                        ]
-                launch(a)
+        def move(a, launch):
+            launch(cells_of(val, a * COLS_B, COLS_B), pl.ds(lax.rem(a, 6) * COLS_B, COLS_B))
+
+        mine_out = pl.ds(pl.multiple_of(half * CELL, 8), CELL)
+
+        def far(src, to):
+            remote(src, out_hbm.at[to, mine_out], out_s, out_r, partner).start()
+
+        def near(src, to):
+            pltpu.make_async_copy(src, out_hbm.at[to, mine_out], out_sem).start()
+
+        for first, launch in ((other * 6, far), (half * 6, near)):
+            def body(n, carry, first=first, launch=launch):
+                new_line(first + n, dt, coef)
+
+                @pl.when(n > 0)
+                def _():
+                    move(first + n - 1, launch)
+
                 return carry
 
             lax.fori_loop(0, 6, body, 0)
-
-        def far(a):
-            src, dst = out_copy(stage_other, a, half)
-            remote(src, dst, out_s, out_r, partner).start()
-
-        def near(a):
-            src, dst = out_copy(stage_own, a, half)
-            pltpu.make_async_copy(src, dst, out_sem).start()
-
-        rows(other * 6, stage_other, far)
-        rows(half * 6, stage_own, near)
-        done = pltpu.make_async_copy(stage_own, lanes_of(out_hbm, half), out_sem)
-        done.wait()
-        sent = remote(stage_other, lanes_of(out_hbm, other), out_s, out_r, partner)
+            move(first + 5, launch)
+        pltpu.make_async_copy(
+            cells_of(val, half * 36, 36), part_of(out_hbm, half), out_sem
+        ).wait()
+        sent = remote(
+            cells_of(val, other * 36, 36), part_of(out_hbm, other), out_s, out_r, partner
+        )
         sent.wait_send()
         sent.wait_recv()
+
+    def bounds():
+        def body(n, carry):
+            for i in range(6):
+                where = pl.ds(pl.multiple_of(48 * n + 8 * i, 8), 8)
+                hi[where] = jnp.where(mask_t[where] == 1, -0.5, BIG)
+                lo[where] = jnp.where(mask_o[where] == 1, 0.5, -BIG)
+            return carry
+
+        lax.fori_loop(0, TOTAL // 48, body, 0)
+
+    def own_cols(a, carry):
+        start_cols(half * 6 + a)
+        return carry
+
+    def other_cols(a, carry):
+        start_cols(other * 6 + a)
+        return carry
+
+    lax.fori_loop(0, 6, own_cols, 0)
+    greet(0)
+    early = along_planes(0, 4, zero)
+    met_all(0)
+    greet(1)
+    swaps[0].wait_recv()
+    lax.fori_loop(0, 6, other_cols, 0)
+    start_low()
+    start_high()
 
     for step in range(STEPS):
         to_transposed()
         pack_side()
         start_side()
-        start_halos()
         if step == 0:
             swaps[1].start()
-            swaps[2].start()
-        peak_p = along_planes()
+            peak_p = along_planes(4, 9, early)
+            met_all(1)
+            greet(2)
+        else:
+            peak_p = along_planes(0, 9, zero)
         peak_4 = along_fourth()
+        if step == 0:
+            met_all(2)
+            greet(3)
+        whole(ghost_al, 0).wait_recv()
+        whole(ghost_ah, 1).wait_recv()
+        peak_a = along_rows()
+        if step == 0:
+            met_all(3)
+            greet(4)
+        whole(ghost_bl, 2).wait_recv()
+        whole(ghost_bh, 3).wait_recv()
+        peak_b = along_cols()
+        if step == 0:
+            met_all(4)
+            greet(5)
         whole(side_in, 4).wait_recv()
         merge_side()
         peak_3 = along_third()
-        whole(ghost_bl, 2).wait_recv()
-        whole(ghost_bh, 3).wait_recv()
-        peak_b = along_cols()
-        whole(ghost_al, 0).wait_recv()
-        whole(ghost_ah, 1).wait_recv()
-        peak_a = along_rows()
+        if step == 0:
+            met_all(5)
         speeds(step, [peak_p, peak_a, peak_b, peak_3, peak_4])
         for k, ref in enumerate(halo_refs):
             whole(ref, k).wait_send()
         if step == 0:
+            swaps[2].start()
+        dt, coef = all_speeds(step)
+        from_transposed(dt, coef)
+        if step == 0:
             for k in (1, 2):
                 locals_[k].wait()
-            spread(owns[1], half * 6, (hi, -0.5, BIG))
-            spread(owns[2], half * 6, (lo, 0.5, -BIG))
-            for k in (1, 2):
                 swaps[k].wait_recv()
-            spread(others[1], other * 6, (hi, -0.5, BIG))
-            spread(others[2], other * 6, (lo, 0.5, -BIG))
+            bounds()
             for k in range(3):
                 swaps[k].wait_send()
-        dt, coef = all_speeds(step)
-        from_transposed(dt, coef)
         if step < STEPS - 1:
             update(dt, coef)
         else:
             last_update(dt, coef)
 
 
+def to_rows(x):
+    x = x.transpose(1, 2, 0, 3).reshape(6, 6, PLANES, 12, 128)
+    return x.transpose(0, 1, 3, 2, 4).reshape(36, 48, 128)
+
+
+def from_rows(x):
+    x = x.reshape(6, 6, 12, PLANES, 128).transpose(0, 1, 3, 2, 4)
+    return x.reshape(6, 6, PLANES, 1536).transpose(2, 0, 1, 3)
+
+
 def solution(mesh):
     def rows(n):
         return pltpu.VMEM((n, 128), F32)
 
     dma = pltpu.SemaphoreType.DMA
-    stage = (PLANES, 6, 6, 768)
     trans = GROUPS * 8 * PITCH
     scratch = [
-        rows(PADDED), rows(TOTAL), rows(TOTAL), rows(TOTAL), rows(TOTAL), rows(PADDED),
+        rows(TOTAL), rows(TOTAL), rows(TOTAL), rows(TOTAL), rows(TOTAL), rows(TOTAL),
         rows(TOTAL), rows(TOTAL),
         rows(3 * LINE), rows(3 * LINE), rows(ROWS_A * 72), rows(ROWS_A * 72),
         rows(GROUPS * SLOTS * PITCH), rows(trans), rows(trans), rows(trans),
         rows(432), rows(432),
-        pltpu.VMEM(stage, F32), pltpu.VMEM(stage, F32),
-        pltpu.VMEM((2,) + stage, jnp.int32), pltpu.VMEM((2,) + stage, jnp.int32),
+        pltpu.VMEM((TOTAL, 128), jnp.int32), pltpu.VMEM((TOTAL, 128), jnp.int32),
         rows(24), rows(24), rows(8 * ROWS_A), rows(72), rows(8 * CHUNKS),
         rows(8 * GROUPS), rows(8 * GROUPS),
         pltpu.VMEM((STEPS, 1, 128), F32), pltpu.VMEM((STEPS, 128, 1, 128), F32),
+        pltpu.SemaphoreType.REGULAR((6,)),
         dma((3,)), dma((3,)), dma((3,)), dma((5,)), dma((5,)), dma((STEPS,)), dma((STEPS,)),
         dma(()), dma(()), dma(()),
     ]
@@ -610,19 +700,23 @@
     def body(value_field, target_mask, obstacle_mask, drift_gains, control_costs):
         anywhere = pl.BlockSpec(memory_space=pl.ANY)
         scalars = pl.BlockSpec(memory_space=pltpu.SMEM)
-        return pl.pallas_call(
+        moved, steps = pl.pallas_call(
             kernel,
             out_shape=(
-                jax.ShapeDtypeStruct(value_field.shape, F32),
+                jax.ShapeDtypeStruct((36, 48, 128), F32),
                 jax.ShapeDtypeStruct((STEPS,), F32),
             ),
             in_specs=[anywhere, anywhere, anywhere, scalars, scalars],
             out_specs=(anywhere, scalars),
             scratch_shapes=scratch,
             compiler_params=pltpu.CompilerParams(
-                has_side_effects=True, vmem_limit_bytes=56 * 2**20
+                collective_id=0, has_side_effects=True, vmem_limit_bytes=56 * 2**20
             ),
-        )(value_field, target_mask, obstacle_mask, drift_gains, control_costs)
+        )(
+            to_rows(value_field), to_rows(target_mask), to_rows(obstacle_mask),
+            drift_gains, control_costs,
+        )
+        return from_rows(moved), steps
 
     grid = P(None, "gx", "gy", None)
     return jax.shard_map(

time: 146 us -> 116 us (0.79)
  Pallas kernels: 137 us -> 107 us
    pallas_call x1, Pallas kernels: 137 us -> 107 us  [body(): pl.pallas_call(kernel, out_shape=(jax.ShapeDtypeStruct((36, 48, 128), F32...]
    transpose x0 -> x3, local copies, waits for them, and re-layouts: none -> 3.87 us  [to_rows(): return x.transpose(0, 1, 3, 2, 4).reshape(36, 48, 128)]
    unnamed x10 -> x8, local copies, waits for them, and re-layouts: 5.72 us -> 2.66 us
    pallas_call x1 -> x0, local copies, waits for them, and re-layouts: 2.75 us -> none  [body(): pl.pallas_call(kernel, out_shape=(jax.ShapeDtypeStruct(value_field.shape,...]
    reshape x0 -> x3, local copies, waits for them, and re-layouts: none -> 2.53 us  [to_rows(): x = x.transpose(1, 2, 0, 3).reshape(6, 6, PLANES, 12, 128)]
where the time goes in v1:
time: 116 us
  Pallas kernels  107 us (92%)
  local copies, waits for them, and re-layouts  9.07 us (8%)
    pallas_call x1, Pallas kernels, body(): pl.pallas_call(kernel, out_shape=(jax.ShapeDtypeStruct((36, 48, 128), F32...  107 us
    transpose x3, local copies, waits for them, and re-layouts, to_rows(): return x.transpose(0, 1, 3, 2, 4).reshape(36, 48, 128)  3.87 us
    unnamed x8, local copies, waits for them, and re-layouts  2.66 us
    reshape x3, local copies, waits for them, and re-layouts, to_rows(): x = x.transpose(1, 2, 0, 3).reshape(6, 6, PLANES, 12, 128)  2.53 us

profile of v1, /device:TPU:1, one launch (start us, length us, event | category | flops | bytes accessed | tf_op | source)
XLA Modules:
  0.0 116.3 jit_solution(10375522619188821368)
XLA Ops:
  0.6 1.6 %reshape.28 = f32[6,6,4,12,128]{4,3,2,1,0:T(8,128)S(1)} reshape(f32[6,6,4,1536]{3,2,1,0:T(4,128)} %bitcast.23) | data formatting | bytes 1769472 | tf_op jit(solution)/shard_map/reshape | solution.py:670
  2.3 0.0 copy-start
  2.3 1.3 %copy.10 = f32[6,6,12,4,128]{4,3,2,1,0:T(4,128)} copy(f32[6,6,12,4,128]{4,2,3,1,0:T(8,128)S(1)} %bitcast.16) | data formatting | bytes 1769472 | tf_op jit(solution)/shard_map/transpose | solution.py:671
  3.5 0.0 copy-done
  3.5 0.5 reshape.30
  4.0 0.0 copy-start.1
  4.0 1.3 %copy.11 = s32[6,6,12,4,128]{4,3,2,1,0:T(4,128)} copy(s32[6,6,12,4,128]{4,2,3,1,0:T(8,128)S(1)} %bitcast.17) | data formatting | bytes 1769472 | tf_op jit(solution)/shard_map/transpose | solution.py:671
  5.3 0.0 copy-done.1
  5.3 0.5 reshape.32
  5.8 1.3 %copy.12 = s32[6,6,12,4,128]{4,3,2,1,0:T(4,128)} copy(s32[6,6,12,4,128]{4,2,3,1,0:T(8,128)S(1)} %bitcast.18) | data formatting | bytes 1769472 | tf_op jit(solution)/shard_map/transpose | solution.py:671
  7.1 106.5 %shard_map.68 = (f32[36,48,128]{2,1,0:T(8,128)}, f32[3]{0:T(128)}) custom-call(f32[36,48,128]{2,1,0:T(8,128)} %bitcast.19, s32[36,48,128]{2,1,0:T(8,128)} %bitcast.20, s32[36,48,128]{2,1,0:T(8,128)} %bitcast.21, f32[5]{0:T(128)} %gains.1, f32[5]{0:T(128)} %costs.1), custom_call_target="tpu_custom_call" | custom-call | tf_op jit(solution)/shard_map/pallas_call | solution.py:703
  113.6 0.0 copy-start.2
  113.6 2.1 %copy.15 = f32[4,6,6,1536]{3,0,2,1:T(4,128)} copy(f32[4,6,6,1536]{3,0,2,1:T(4,128)} %bitcast.22) | data formatting | bytes 1769472
  115.8 0.0 copy-done.2
  115.8 0.5 copy.16
Async XLA Ops:
  2.3 1.3 %copy-start = (s32[4,6,6,1536]{3,0,2,1:T(4,128)S(1)}, s32[4,6,6,1536]{3,0,2,1:T(4,128)}, u32[]{:S(2)}) copy-start(s32[4,6,6,1536]{3,0,2,1:T(4,128)} %param.6) | copy-start | bytes 2654212
  4.0 1.3 %copy-start.1 = (s32[4,6,6,1536]{3,0,2,1:T(4,128)S(1)}, s32[4,6,6,1536]{3,0,2,1:T(4,128)}, u32[]{:S(2)}) copy-start(s32[4,6,6,1536]{3,0,2,1:T(4,128)} %param.7) | copy-start | bytes 2654212
  113.6 2.1 %copy-start.2 = (f32[3]{0:T(128)S(1)}, f32[3]{0:T(128)}, u32[]{:S(2)}) copy-start(f32[3]{0:T(128)} %get-tuple-element.9) | copy-start | bytes 40

commit v2 on v1

--- a/solution.py
+++ b/solution.py
@@ -6,6 +6,7 @@
 from jax import lax
 from jax.experimental import pallas as pl
 from jax.experimental.pallas import tpu as pltpu
+from jax.experimental.layout import Layout, with_layout_constraint
 from jax.sharding import PartitionSpec as P
 
 PLANES, N3, N4, GRID, STEPS, NA, NB = 4, 32, 48, 96, 3, 48, 96
@@ -288,12 +289,9 @@
                 row = tr_row(g, GHOST + merged // N4) + merged % N4
                 tr[pl.ds(row, 8)] = block[8 * k:8 * k + 8]
 
-        def body(g, carry):
+        for g in range(GROUPS - 1):
             for r in range(3):
                 put(g, r, val[pl.ds(r * PLANES + g, 128, stride=12)].T)
-            return carry
-
-        lax.fori_loop(0, GROUPS - 1, body, 0)
         for r in range(3):
             parts = [
                 val[pl.ds(1536 + r * PLANES + p, 16, stride=12)] for p in range(PLANES)
@@ -317,7 +315,7 @@
                     )
             return carry
 
-        lax.fori_loop(0, 3, body, 0)
+        lax.fori_loop(0, 3, body, 0, unroll=True)
 
     def merge_side():
         def body(g, carry):
@@ -341,7 +339,7 @@
                     )
             return carry
 
-        lax.fori_loop(0, GROUPS, body, 0)
+        lax.fori_loop(0, GROUPS, body, 0, unroll=True)
 
     def cell_out(left, right, flow, square, factor, peak):
         total = left + right
@@ -372,7 +370,7 @@
                 hn[rows[p]] = part
             return peak
 
-        return lax.fori_loop(first * CHUNKS, end * CHUNKS, body, peak)
+        return lax.fori_loop(first * CHUNKS, end * CHUNKS, body, peak, unroll=2)
 
     def along_rows():
         def body(n, peak):
@@ -391,7 +389,7 @@
                 hn[where] += part
             return peak
 
-        return lax.fori_loop(0, LINE // 8, body, zero)
+        return lax.fori_loop(0, LINE // 8, body, zero, unroll=1)
 
     def along_cols():
         def body(n, peak):
@@ -414,7 +412,7 @@
                 hn[where] += part
             return peak
 
-        return lax.fori_loop(0, 3 * ROWS_A, body, zero)
+        return lax.fori_loop(0, 3 * ROWS_A, body, zero, unroll=2)
 
     def along_third():
         def body(n, peak):
@@ -429,7 +427,7 @@
                 ht[where] += part
             return peak
 
-        return lax.fori_loop(0, GROUPS * 6, body, zero)
+        return lax.fori_loop(0, GROUPS * 6, body, zero, unroll=2)
 
     slope4 = fscale[4] * cell
 
@@ -455,7 +453,7 @@
                 ht[where] = part
             return peak
 
-        return lax.fori_loop(0, GROUPS * 4, body, zero)
+        return lax.fori_loop(0, GROUPS * 4, body, zero, unroll=1)
 
     def greet(k):
         if k < len(ROUNDS):
@@ -511,12 +509,9 @@
                 parts.append(coef[3] * d_3[where] + coef[4] * d_4[where] - dt * ht[where])
             return jnp.concatenate(parts, axis=0).T
 
-        def body(g, carry):
+        for g in range(GROUPS - 1):
             for r in range(3):
                 wn[pl.ds(r * PLANES + g, 128, stride=12)] = take(g, r)
-            return carry
-
-        lax.fori_loop(0, GROUPS - 1, body, 0)
         for r in range(3):
             block = take(GROUPS - 1, r)
             for p in range(PLANES):
@@ -668,6 +663,7 @@
 
 def to_rows(x):
     x = x.transpose(1, 2, 0, 3).reshape(6, 6, PLANES, 12, 128)
+    x = with_layout_constraint(x, Layout((0, 1, 3, 2, 4)))
     return x.transpose(0, 1, 3, 2, 4).reshape(36, 48, 128)
 
 

time: 116 us -> 107 us (0.922)
  local copies, waits for them, and re-layouts: 9.07 us -> 2.65 us
  Pallas kernels: 107 us -> 104 us
    transpose x3 -> x0, local copies, waits for them, and re-layouts: 3.87 us -> none  [to_rows(): return x.transpose(0, 1, 3, 2, 4).reshape(36, 48, 128)]
    pallas_call x1, Pallas kernels: 107 us -> 104 us  [body(): pl.pallas_call(kernel, out_shape=(jax.ShapeDtypeStruct((36, 48, 128), F32...]
    reshape x3 -> x0, local copies, waits for them, and re-layouts: 2.53 us -> none  [to_rows(): x = x.transpose(1, 2, 0, 3).reshape(6, 6, PLANES, 12, 128)]
    unnamed x8 -> x4, local copies, waits for them, and re-layouts: 2.66 us -> 2.65 us
where the time goes in v2:
time: 107 us
  Pallas kernels  104 us (97%)
  local copies, waits for them, and re-layouts  2.65 us (2%)
    pallas_call x1, Pallas kernels, body(): pl.pallas_call(kernel, out_shape=(jax.ShapeDtypeStruct((36, 48, 128), F32...  104 us
    unnamed x4, local copies, waits for them, and re-layouts  2.65 us

profile of v2, /device:TPU:1, one launch (start us, length us, event | category | flops | bytes accessed | tf_op | source)
XLA Modules:
  0.0 107.1 jit_solution(4783711990395532917)
XLA Ops:
  0.6 103.8 %shard_map.68 = (f32[36,48,128]{2,1,0:T(8,128)}, f32[3]{0:T(128)}) custom-call(f32[36,48,128]{2,1,0:T(8,128)} %bitcast.28, s32[36,48,128]{2,1,0:T(8,128)} %bitcast.29, s32[36,48,128]{2,1,0:T(8,128)} %bitcast.30, f32[5]{0:T(128)} %gains.1, f32[5]{0:T(128)} %costs.1), custom_call_target="tpu_custom_call" | custom-call | tf_op jit(solution)/shard_map/pallas_call | solution.py:699
  104.5 0.0 copy-start
  104.5 2.1 %copy.9 = f32[4,6,6,1536]{3,0,2,1:T(4,128)} copy(f32[4,6,6,1536]{3,0,2,1:T(4,128)} %bitcast.31) | data formatting | bytes 1769472
  106.6 0.0 copy-done
  106.6 0.5 copy.10
Async XLA Ops:
  104.5 2.1 %copy-start = (f32[3]{0:T(128)S(1)}, f32[3]{0:T(128)}, u32[]{:S(2)}) copy-start(f32[3]{0:T(128)} %get-tuple-element.9) | copy-start | bytes 40

commit v3 on v2

--- a/solution.py
+++ b/solution.py
@@ -24,6 +24,7 @@
 SLOTS = 14
 GHOST = 3
 EPS = 0.75e-6
+EARLY = 18
 
 
 def _hops(offset):
@@ -36,6 +37,10 @@
     [(dx, dy) for dx in range(8) for dy in range(16) if dx or dy], key=_hops, reverse=True
 )
 ROUNDS = (((0, 1), (0, 15)), ((0, 2), (0, 14)), ((0, 4), (0, 12)), ((2, 0), (6, 0)), ((4, 0),))
+
+
+def line_order(n):
+    return jnp.where(n < 6, jnp.where(n < 3, n, n + 6), n - 3)
 
 
 def _add(x, y):
@@ -130,7 +135,7 @@
     mask_t, mask_o,
     tab_f1, tab_f2, tab_sa, tab_ab, tab_x3, tab_l3, tab_l4,
     ar_src, ar_buf,
-    met, local_sem, swap_s, swap_r, halo_s, halo_r, ar_s, ar_r, out_sem, out_s, out_r,
+    met, local_sem, swap_s, swap_r, row_s, row_r, col_s, col_r, side_s, side_r, ar_s, ar_r, out_sem, out_s, out_r,
 ):
     gx, gy = lax.axis_index("gx"), lax.axis_index("gy")
     half = lax.rem(gx, 2)
@@ -161,13 +166,23 @@
     def cells_of(ref, first, count):
         return ref.reshape(TOTAL // CELL, CELL, 128).at[pl.ds(first, count)]
 
+    def target_of(ref, first, count):
+        return ref.at[pl.ds(first, count), pl.ds(pl.multiple_of(other * CELL, 8), CELL)]
+
     swaps = [
         remote(
             part_of(inputs[k], other), cells_of(places[k], half * 36, 36),
             swap_s.at[k], swap_r.at[k], partner,
         )
-        for k in range(3)
+        for k in range(2)
     ]
+    for k, (first, count) in enumerate(((0, EARLY), (EARLY, 36 - EARLY))):
+        swaps.append(
+            remote(
+                target_of(obstacle_hbm, first, count), cells_of(mask_o, half * 36 + first, count),
+                swap_s.at[2 + k], swap_r.at[2 + k], partner,
+            )
+        )
     locals_ = [
         pltpu.make_async_copy(
             part_of(inputs[k], half), cells_of(places[k], half * 36, 36), local_sem.at[k]
@@ -250,34 +265,63 @@
     lax.fori_loop(0, GROUPS, table_lane, 0)
     locals_[0].wait()
 
-    def whole(ref, k):
-        return remote(ref, ref, halo_s.at[k], halo_r.at[k], partner)
-
-    halo_refs = (ghost_al, ghost_ah, ghost_bl, ghost_bh, side_in)
-
     def start_side():
-        remote(side_out, side_in, halo_s.at[4], halo_r.at[4], partner).start()
+        remote(side_out, side_in, side_s, side_r, partner).start()
+
+    def wait_side():
+        remote(side_out, side_in, side_s, side_r, partner).wait_recv()
 
     def start_cols(a):
         at = pl.multiple_of(a * LINE, 8)
         to = pl.ds(pl.multiple_of(a * 72, 8), 72)
         remote(
-            val.at[pl.ds(at + 72, 72)], ghost_bl.at[to], halo_s.at[2], halo_r.at[2], col_after
+            val.at[pl.ds(at + 72, 72)], ghost_bl.at[to], col_s.at[0], col_r.at[0, a], col_after
         ).start()
         remote(
-            val.at[pl.ds(at, 72)], ghost_bh.at[to], halo_s.at[3], halo_r.at[3], col_before
+            val.at[pl.ds(at, 72)], ghost_bh.at[to], col_s.at[1], col_r.at[1, a], col_before
         ).start()
 
+    def lines_of(ref, first, b):
+        return ref.reshape(ref.shape[0] // LINE, LINE, 128).at[
+            pl.ds(first, 3), pl.ds(pl.multiple_of(b * CELL, 8), CELL)
+        ]
+
+    def start_edge(k):
+        first, ghost, device = (
+            (ROWS_A - 3, ghost_al, row_after), (0, ghost_ah, row_before)
+        )[k]
+
+        def body(b, carry):
+            remote(
+                lines_of(val, first, b), lines_of(ghost, 0, b),
+                row_s.at[k], row_r.at[k, b], device,
+            ).start()
+            return carry
+
+        lax.fori_loop(0, COLS_B, body, 0)
+
     def start_high():
-        remote(
-            val.at[pl.ds((ROWS_A - 3) * LINE, 3 * LINE)], ghost_al,
-            halo_s.at[0], halo_r.at[0], row_after,
-        ).start()
+        start_edge(0)
 
     def start_low():
-        remote(
-            val.at[pl.ds(0, 3 * LINE)], ghost_ah, halo_s.at[1], halo_r.at[1], row_before
-        ).start()
+        start_edge(1)
+
+    def wait_rows(b):
+        for k, ghost in enumerate((ghost_al, ghost_ah)):
+            piece = lines_of(ghost, 0, b)
+            remote(piece, piece, row_s.at[k], row_r.at[k, b], partner).wait_recv()
+
+    def wait_cols(a):
+        for k, ghost in enumerate((ghost_bl, ghost_bh)):
+            piece = ghost.at[pl.ds(pl.multiple_of(a * 72, 8), 72)]
+            remote(piece, piece, col_s.at[k], col_r.at[k, a], partner).wait_recv()
+
+    def sent_halos():
+        for k, ghost in enumerate((ghost_al, ghost_ah)):
+            remote(ghost, ghost, row_s.at[k], row_r.at[k, 0], partner).wait_send()
+        for k, ghost in enumerate((ghost_bl, ghost_bh)):
+            remote(ghost, ghost, col_s.at[k], col_r.at[k, 0], partner).wait_send()
+        remote(side_out, side_in, side_s, side_r, partner).wait_send()
 
     def tr_row(g, slot):
         return g * (SLOTS * PITCH) + slot * PITCH
@@ -304,42 +348,52 @@
     mine = jnp.where(is_low, lane8 & 1, 1 - (lane8 & 1)) == 0
     send_slot = jnp.where(is_low, GHOST + 5, GHOST)
 
+    low_lanes = lane8 < 64
+    SIDE = [(t, q) for t in range(3) for q in range(6)]
+
     def pack_side():
-        def body(k, carry):
-            for s in range(3):
-                for q in range(6):
-                    one = tr[pl.ds(tr_row(2 * k, send_slot + s) + 8 * q, 8)]
-                    two = tr[pl.ds(tr_row(jnp.minimum(2 * k + 1, 4), send_slot + s) + 8 * q, 8)]
-                    side_out[pl.ds(k * 144 + s * 48 + 8 * q, 8)] = jnp.where(
-                        mine, pltpu.roll(one, turn, 1), two
-                    )
-            return carry
-
-        lax.fori_loop(0, 3, body, 0, unroll=True)
+        def part(g, v):
+            t, q = SIDE[v]
+            return tr[pl.ds(tr_row(g, send_slot + t) + 8 * q, 8)]
+
+        def pair(one, two):
+            return jnp.where(mine, pltpu.roll(one, turn, 1), two)
+
+        for k in range(2):
+            for v in range(18):
+                side_out[pl.ds(k * 144 + 8 * v, 8)] = pair(part(2 * k, v), part(2 * k + 1, v))
+        for w in range(5):
+            group = [part(4, min(4 * w + i, 17)) for i in range(4)]
+            side_out[pl.ds(288 + 8 * w, 8)] = jnp.where(
+                low_lanes, pair(group[0], group[1]), pltpu.roll(pair(group[2], group[3]), 64, 1)
+            )
 
     def merge_side():
-        def body(g, carry):
-            pack = lax.div(g, 2)
-            second = lax.rem(g, 2) == 1
-            back = jnp.where(is_low, 1, 127)
-            for s in range(3):
-                for q in range(6):
-                    at = 8 * q
-                    got = side_in[pl.ds(pack * 144 + s * 48 + at, 8)]
-                    got = jnp.where(second, pltpu.roll(got, back, 1), got)
-                    top = tr[pl.ds(tr_row(g, GHOST + 7) + at, 8)]
-                    bottom = tr[pl.ds(tr_row(g, GHOST) + at, 8)]
-                    up = pltpu.roll(tr[pl.ds(tr_row(g, GHOST + s) + at, 8)], 127, 1)
-                    down = pltpu.roll(tr[pl.ds(tr_row(g, GHOST + 5 + s) + at, 8)], 1, 1)
-                    tr[pl.ds(tr_row(g, GHOST + 8 + s) + at, 8)] = jnp.where(
-                        odd, jnp.where(is_low, got, top), up
-                    )
-                    tr[pl.ds(tr_row(g, s) + at, 8)] = jnp.where(
-                        odd, down, jnp.where(is_low, bottom, got)
-                    )
-            return carry
-
-        lax.fori_loop(0, GROUPS, body, 0, unroll=True)
+        back = jnp.where(is_low, 1, 127)
+        for g in range(GROUPS):
+            for v, (t, q) in enumerate(SIDE):
+                at = 8 * q
+                if g < 4:
+                    got = side_in[pl.ds((g // 2) * 144 + 8 * v, 8)]
+                    second = g % 2
+                else:
+                    got = side_in[pl.ds(288 + 8 * (v // 4), 8)]
+                    second = v % 2
+                    if v % 4 > 1:
+                        got = pltpu.roll(got, 64, 1)
+                    got = jnp.where(low_lanes, got, 0.0)
+                if second:
+                    got = pltpu.roll(got, back, 1)
+                top = tr[pl.ds(tr_row(g, GHOST + 7) + at, 8)]
+                bottom = tr[pl.ds(tr_row(g, GHOST) + at, 8)]
+                up = pltpu.roll(tr[pl.ds(tr_row(g, GHOST + t) + at, 8)], 127, 1)
+                down = pltpu.roll(tr[pl.ds(tr_row(g, GHOST + 5 + t) + at, 8)], 1, 1)
+                tr[pl.ds(tr_row(g, GHOST + 8 + t) + at, 8)] = jnp.where(
+                    odd, jnp.where(is_low, got, top), up
+                )
+                tr[pl.ds(tr_row(g, t) + at, 8)] = jnp.where(
+                    odd, down, jnp.where(is_low, bottom, got)
+                )
 
     def cell_out(left, right, flow, square, factor, peak):
         total = left + right
@@ -372,47 +426,55 @@
 
         return lax.fori_loop(first * CHUNKS, end * CHUNKS, body, peak, unroll=2)
 
-    def along_rows():
-        def body(n, peak):
-            at = pl.multiple_of(8 * n, 8)
-            line = (
-                [ghost_al[pl.ds(i * LINE + at, 8)] for i in range(3)]
-                + [val[pl.ds(a * LINE + at, 8)] for a in range(ROWS_A)]
-                + [ghost_ah[pl.ds(i * LINE + at, 8)] for i in range(3)]
-            )
-            flow = tab_f1[pl.ds(pl.multiple_of(8 * lax.rem(n, 3), 8), 8)]
-            square = flow * flow
-            for a, (left, right) in enumerate(chain(line)):
-                gap, part, peak = cell_out(left, right, flow, square, kk[1], peak)
-                where = pl.ds(a * LINE + at, 8)
-                d_a[where] = gap
-                hn[where] += part
-            return peak
-
-        return lax.fori_loop(0, LINE // 8, body, zero, unroll=1)
-
-    def along_cols():
-        def body(n, peak):
-            a, j = lax.div(n, 3), lax.rem(n, 3)
-            ghost = pl.multiple_of(a * 72 + 8 * j, 8)
-            at = pl.multiple_of(a * LINE + 8 * j, 8)
-            line = (
-                [ghost_bl[pl.ds(ghost + i * CELL, 8)] for i in range(3)]
-                + [val[pl.ds(at + b * CELL, 8)] for b in range(COLS_B)]
-                + [ghost_bh[pl.ds(ghost + i * CELL, 8)] for i in range(3)]
-            )
-            flow = tab_f2[pl.ds(pl.multiple_of(8 * j, 8), 8)] + tab_sa[
-                pl.ds(pl.multiple_of(8 * a, 8), 8)
-            ]
-            square = flow * flow
-            for b, (left, right) in enumerate(chain(line)):
-                gap, part, peak = cell_out(left, right, flow, square, kk[2], peak)
-                where = pl.ds(at + b * CELL, 8)
-                d_b[where] = gap
-                hn[where] += part
-            return peak
-
-        return lax.fori_loop(0, 3 * ROWS_A, body, zero, unroll=2)
+    def row_chain(n, peak):
+        at = pl.multiple_of(8 * n, 8)
+        line = (
+            [ghost_al[pl.ds(i * LINE + at, 8)] for i in range(3)]
+            + [val[pl.ds(a * LINE + at, 8)] for a in range(ROWS_A)]
+            + [ghost_ah[pl.ds(i * LINE + at, 8)] for i in range(3)]
+        )
+        flow = tab_f1[pl.ds(pl.multiple_of(8 * lax.rem(n, 3), 8), 8)]
+        square = flow * flow
+        for a, (left, right) in enumerate(chain(line)):
+            gap, part, peak = cell_out(left, right, flow, square, kk[1], peak)
+            where = pl.ds(a * LINE + at, 8)
+            d_a[where] = gap
+            hn[where] += part
+        return peak
+
+    def col_chain(a, j, peak):
+        ghost = pl.multiple_of(a * 72 + 8 * j, 8)
+        at = pl.multiple_of(a * LINE + 8 * j, 8)
+        line = (
+            [ghost_bl[pl.ds(ghost + i * CELL, 8)] for i in range(3)]
+            + [val[pl.ds(at + b * CELL, 8)] for b in range(COLS_B)]
+            + [ghost_bh[pl.ds(ghost + i * CELL, 8)] for i in range(3)]
+        )
+        flow = tab_f2[pl.ds(pl.multiple_of(8 * j, 8), 8)] + tab_sa[
+            pl.ds(pl.multiple_of(8 * a, 8), 8)
+        ]
+        square = flow * flow
+        for b, (left, right) in enumerate(chain(line)):
+            gap, part, peak = cell_out(left, right, flow, square, kk[2], peak)
+            where = pl.ds(at + b * CELL, 8)
+            d_b[where] = gap
+            hn[where] += part
+        return peak
+
+    def along_edges():
+        def body(k, peaks):
+            row_peak, col_peak = peaks
+            wait_rows(k)
+            for j in range(3):
+                row_peak = row_chain(3 * k + j, row_peak)
+            for i in range(2):
+                a = line_order(2 * k + i)
+                wait_cols(a)
+                for j in range(3):
+                    col_peak = col_chain(a, j, col_peak)
+            return row_peak, col_peak
+
+        return lax.fori_loop(0, COLS_B, body, (zero, zero))
 
     def along_third():
         def body(n, peak):
@@ -525,8 +587,7 @@
             val[where] = jnp.maximum(jnp.minimum(moved, hi[where]), lo[where])
 
     def update(dt, coef):
-        def line_of(n):
-            return jnp.where(n < 6, jnp.where(n < 3, n, n + 6), n - 3)
+        line_of = line_order
 
         def body(n, carry):
             new_line(line_of(n), dt, coef)
@@ -581,15 +642,15 @@
         sent.wait_send()
         sent.wait_recv()
 
-    def bounds():
+    def bounds(which):
         def body(n, carry):
-            for i in range(6):
-                where = pl.ds(pl.multiple_of(48 * n + 8 * i, 8), 8)
+            for i in range(9):
+                where = pl.ds(pl.multiple_of(which * (TOTAL // 2) + 72 * n + 8 * i, 8), 8)
                 hi[where] = jnp.where(mask_t[where] == 1, -0.5, BIG)
                 lo[where] = jnp.where(mask_o[where] == 1, 0.5, -BIG)
             return carry
 
-        lax.fori_loop(0, TOTAL // 48, body, 0)
+        lax.fori_loop(0, TOTAL // 144, body, 0)
 
     def own_cols(a, carry):
         start_cols(half * 6 + a)
@@ -615,6 +676,7 @@
         start_side()
         if step == 0:
             swaps[1].start()
+            swaps[2].start()
             peak_p = along_planes(4, 9, early)
             met_all(1)
             greet(2)
@@ -624,36 +686,32 @@
         if step == 0:
             met_all(2)
             greet(3)
-        whole(ghost_al, 0).wait_recv()
-        whole(ghost_ah, 1).wait_recv()
-        peak_a = along_rows()
+        peak_a, peak_b = along_edges()
         if step == 0:
             met_all(3)
             greet(4)
-        whole(ghost_bl, 2).wait_recv()
-        whole(ghost_bh, 3).wait_recv()
-        peak_b = along_cols()
+        wait_side()
+        merge_side()
         if step == 0:
             met_all(4)
             greet(5)
-        whole(side_in, 4).wait_recv()
-        merge_side()
         peak_3 = along_third()
         if step == 0:
             met_all(5)
         speeds(step, [peak_p, peak_a, peak_b, peak_3, peak_4])
-        for k, ref in enumerate(halo_refs):
-            whole(ref, k).wait_send()
+        sent_halos()
         if step == 0:
-            swaps[2].start()
+            swaps[3].start()
+            for k in (1, 2):
+                locals_[k].wait()
+            bounds(half)
         dt, coef = all_speeds(step)
         from_transposed(dt, coef)
         if step == 0:
-            for k in (1, 2):
-                locals_[k].wait()
+            for k in (1, 2, 3):
                 swaps[k].wait_recv()
-            bounds()
-            for k in range(3):
+            bounds(other)
+            for k in range(4):
                 swaps[k].wait_send()
         if step < STEPS - 1:
             update(dt, coef)
@@ -683,13 +741,15 @@
         rows(TOTAL), rows(TOTAL),
         rows(3 * LINE), rows(3 * LINE), rows(ROWS_A * 72), rows(ROWS_A * 72),
         rows(GROUPS * SLOTS * PITCH), rows(trans), rows(trans), rows(trans),
-        rows(432), rows(432),
+        rows(328), rows(328),
         pltpu.VMEM((TOTAL, 128), jnp.int32), pltpu.VMEM((TOTAL, 128), jnp.int32),
         rows(24), rows(24), rows(8 * ROWS_A), rows(72), rows(8 * CHUNKS),
         rows(8 * GROUPS), rows(8 * GROUPS),
         pltpu.VMEM((STEPS, 1, 128), F32), pltpu.VMEM((STEPS, 128, 1, 128), F32),
         pltpu.SemaphoreType.REGULAR((6,)),
-        dma((3,)), dma((3,)), dma((3,)), dma((5,)), dma((5,)), dma((STEPS,)), dma((STEPS,)),
+        dma((3,)), dma((4,)), dma((4,)),
+        dma((2,)), dma((2, COLS_B)), dma((2,)), dma((2, ROWS_A)), dma(()), dma(()),
+        dma((STEPS,)), dma((STEPS,)),
         dma(()), dma(()), dma(()),
     ]
 
@@ -706,7 +766,7 @@
             out_specs=(anywhere, scalars),
             scratch_shapes=scratch,
             compiler_params=pltpu.CompilerParams(
-                collective_id=0, has_side_effects=True, vmem_limit_bytes=56 * 2**20
+                collective_id=0, has_side_effects=True, vmem_limit_bytes=53 * 2**20
             ),
         )(
             to_rows(value_field), to_rows(target_mask), to_rows(obstacle_mask),

time: 107 us -> 103 us (0.963)
  Pallas kernels: 104 us -> 99.7 us
    pallas_call x1, Pallas kernels: 104 us -> 99.7 us  [body(): pl.pallas_call(kernel, out_shape=(jax.ShapeDtypeStruct((36, 48, 128), F32...]
    unnamed x4 -> x6, local copies, waits for them, and re-layouts: 2.65 us -> 2.08 us
where the time goes in v3:
time: 103 us; the launch traced here: 102 us
  Pallas kernels  99.7 us (97%)
  local copies, waits for them, and re-layouts  2.08 us (2%)
    pallas_call x1, Pallas kernels, body(): pl.pallas_call(kernel, out_shape=(jax.ShapeDtypeStruct((36, 48, 128), F32...  99.7 us
    unnamed x6, local copies, waits for them, and re-layouts  2.08 us

profile of v3, /device:TPU:1, one launch (start us, length us, event | category | flops | bytes accessed | tf_op | source)
XLA Modules:
  0.0 102.4 jit_solution(5357058286433106776)
XLA Ops:
  0.6 0.0 copy-start
  0.6 0.0 copy-start.1
  0.7 0.6 copy-done
  1.3 0.0 copy-done.1
  1.3 99.7 %shard_map.68 = (f32[36,48,128]{2,1,0:T(8,128)S(1)}, f32[3]{0:T(128)S(1)}) custom-call(f32[36,48,128]{2,1,0:T(8,128)} %bitcast.29, s32[36,48,128]{2,1,0:T(8,128)} %bitcast.30, s32[36,48,128]{2,1,0:T(8,128)} %bitcast.31, f32[5]{0:T(128)S(1)} %copy-done, f32[5]{0:T(128)S(1)} %copy-done.1), custom_call_target="tpu_custom_call" | custom-call | tf_op jit(solution)/shard_map/pallas_call | solution.py:759
  101.0 0.9 copy.9
  101.9 0.5 copy.10
Async XLA Ops:
  0.6 0.7 copy-start
  0.6 0.7 copy-start.1

commit v4 on v3

--- a/solution.py
+++ b/solution.py
@@ -24,6 +24,7 @@
 SLOTS = 14
 GHOST = 3
 EPS = 0.75e-6
+FIRST = 14
 EARLY = 18
 
 
@@ -131,6 +132,7 @@
     out_hbm, steps_out,
     val, hn, d_a, d_b, d_p, wn, hi, lo,
     ghost_al, ghost_ah, ghost_bl, ghost_bh,
+    r_p, r_a, r_b, r_3, r_4, tab_f0,
     tr, ht, d_3, d_4, side_out, side_in,
     mask_t, mask_o,
     tab_f1, tab_f2, tab_sa, tab_ab, tab_x3, tab_l3, tab_l4,
@@ -174,13 +176,16 @@
             part_of(inputs[k], other), cells_of(places[k], half * 36, 36),
             swap_s.at[k], swap_r.at[k], partner,
         )
-        for k in range(2)
+        for k in range(1)
     ]
-    for k, (first, count) in enumerate(((0, EARLY), (EARLY, 36 - EARLY))):
+    for k, (source, place, first, count) in enumerate((
+        (target_hbm, mask_t, 0, FIRST), (target_hbm, mask_t, FIRST, 36 - FIRST),
+        (obstacle_hbm, mask_o, 0, EARLY), (obstacle_hbm, mask_o, EARLY, 36 - EARLY),
+    )):
         swaps.append(
             remote(
-                target_of(obstacle_hbm, first, count), cells_of(mask_o, half * 36 + first, count),
-                swap_s.at[2 + k], swap_r.at[2 + k], partner,
+                target_of(source, first, count), cells_of(place, half * 36 + first, count),
+                swap_s.at[1 + k], swap_r.at[1 + k], partner,
             )
         )
     locals_ = [
@@ -193,6 +198,7 @@
         locals_[k].start()
     pl.semaphore_wait(barrier, 5)
     swaps[0].start()
+    swaps[1].start()
 
     lane8 = lax.broadcasted_iota(jnp.int32, (8, 128), 1)
     lane8f = lane8.astype(F32)
@@ -224,6 +230,7 @@
         x4 = (fourth - N4 / 2 + 0.5) * cell
         tab_f1[pl.ds(8 * block, 8)] = fscale[1] * (x4 - 0.3 * x0)
         tab_f2[pl.ds(8 * block, 8)] = fscale[2] * x3
+        tab_f0[pl.ds(8 * block, 8)] = fscale[0] * x3
     for chunk in range(CHUNKS):
         third, _ = split_lane((half_f * CHUNKS + chunk) * 128.0 + lane8f)
         tab_x3[pl.ds(8 * chunk, 8)] = fscale[0] * ((third - N3 / 2 + 0.5) * cell)
@@ -395,12 +402,11 @@
                     odd, down, jnp.where(is_low, bottom, got)
                 )
 
-    def cell_out(left, right, flow, square, factor, peak):
-        total = left + right
+    def cell_out(left, right, flow, peak):
         gap = right - left
-        rest = flow - total
+        rest = flow - (left + right)
         peak = jnp.maximum(peak, jnp.abs(rest) + jnp.abs(gap))
-        return gap, (square - rest * rest) * factor, peak
+        return gap, rest, peak
 
     zero = jnp.zeros((8, 128), F32)
 
@@ -414,14 +420,13 @@
             flow = tab_ab[pl.ds(pl.multiple_of(8 * q, 8), 8)] + tab_x3[
                 pl.ds(pl.multiple_of(8 * c, 8), 8)
             ]
-            square = flow * flow
             line = [got[0]] * 3 + got + [got[3]] * 3
             for p, (left, right) in enumerate(chain(line)):
                 left = zero if left is None else left
                 right = zero if right is None else right
-                gap, part, peak = cell_out(left, right, flow, square, kk[0], peak)
+                gap, rest, peak = cell_out(left, right, flow, peak)
                 d_p[rows[p]] = gap
-                hn[rows[p]] = part
+                r_p[rows[p]] = rest
             return peak
 
         return lax.fori_loop(first * CHUNKS, end * CHUNKS, body, peak, unroll=2)
@@ -434,12 +439,11 @@
             + [ghost_ah[pl.ds(i * LINE + at, 8)] for i in range(3)]
         )
         flow = tab_f1[pl.ds(pl.multiple_of(8 * lax.rem(n, 3), 8), 8)]
-        square = flow * flow
         for a, (left, right) in enumerate(chain(line)):
-            gap, part, peak = cell_out(left, right, flow, square, kk[1], peak)
+            gap, rest, peak = cell_out(left, right, flow, peak)
             where = pl.ds(a * LINE + at, 8)
             d_a[where] = gap
-            hn[where] += part
+            r_a[where] = rest
         return peak
 
     def col_chain(a, j, peak):
@@ -453,40 +457,43 @@
         flow = tab_f2[pl.ds(pl.multiple_of(8 * j, 8), 8)] + tab_sa[
             pl.ds(pl.multiple_of(8 * a, 8), 8)
         ]
-        square = flow * flow
         for b, (left, right) in enumerate(chain(line)):
-            gap, part, peak = cell_out(left, right, flow, square, kk[2], peak)
+            gap, rest, peak = cell_out(left, right, flow, peak)
             where = pl.ds(at + b * CELL, 8)
             d_b[where] = gap
-            hn[where] += part
+            r_b[where] = rest
         return peak
 
-    def along_edges():
-        def body(k, peaks):
-            row_peak, col_peak = peaks
-            wait_rows(k)
+    def along_rows():
+        def body(b, peak):
+            wait_rows(b)
             for j in range(3):
-                row_peak = row_chain(3 * k + j, row_peak)
+                peak = row_chain(3 * b + j, peak)
+            return peak
+
+        return lax.fori_loop(0, COLS_B, body, zero)
+
+    def along_cols(order):
+        def body(k, peak):
             for i in range(2):
-                a = line_order(2 * k + i)
+                a = order(2 * k + i)
                 wait_cols(a)
                 for j in range(3):
-                    col_peak = col_chain(a, j, col_peak)
-            return row_peak, col_peak
-
-        return lax.fori_loop(0, COLS_B, body, (zero, zero))
+                    peak = col_chain(a, j, peak)
+            return peak
+
+        return lax.fori_loop(0, ROWS_A // 2, body, zero)
 
     def along_third():
         def body(n, peak):
             g, q = lax.div(n, 6), lax.rem(n, 6)
             line = [tr[pl.ds(tr_row(g, s) + 8 * q, 8)] for s in range(SLOTS)]
             flow = tab_l3[pl.ds(pl.multiple_of(8 * g, 8), 8)]
-            square = flow * flow
             for s, (left, right) in enumerate(chain(line)):
-                gap, part, peak = cell_out(left, right, flow, square, kk[3], peak)
+                gap, rest, peak = cell_out(left, right, flow, peak)
                 where = pl.ds((g * 8 + s) * PITCH + 8 * q, 8)
                 d_3[where] = gap
-                ht[where] += part
+                r_3[where] = rest
             return peak
 
         return lax.fori_loop(0, GROUPS * 6, body, zero, unroll=2)
@@ -509,10 +516,10 @@
             base = table - slope4 * (first.astype(F32) - (N4 / 2 - 0.5))
             for i, (left, right) in enumerate(chain(line)):
                 flow = base - slope4 * float(i)
-                gap, part, peak = cell_out(left, right, flow, flow * flow, kk[4], peak)
+                gap, rest, peak = cell_out(left, right, flow, peak)
                 where = pl.ds(g * 8 * PITCH + first + i, 8, stride=PITCH)
                 d_4[where] = gap
-                ht[where] = part
+                r_4[where] = rest
             return peak
 
         return lax.fori_loop(0, GROUPS * 4, body, zero, unroll=1)
@@ -561,6 +568,44 @@
             time_step * speed[i] * (1.0 / (12.0 * SPACING[i])) for i in range(5)
         ]
 
+    def gather_terms():
+        def natural(ab, carry):
+            cos_part = tab_ab[pl.ds(ab, 8, stride=0)]
+            sin_part = tab_sa[pl.ds(pl.multiple_of(8 * lax.div(ab, COLS_B), 8), 8)]
+            for j in range(3):
+                where = pl.ds(pl.multiple_of(ab * CELL + 8 * j, 8), 8)
+                table = pl.ds(8 * j, 8)
+                term = None
+                for k, flow, rest in (
+                    (0, tab_f0[table] + cos_part, r_p[where]),
+                    (1, tab_f1[table], r_a[where]),
+                    (2, tab_f2[table] + sin_part, r_b[where]),
+                ):
+                    part = (flow * flow - rest * rest) * kk[k]
+                    term = part if term is None else term + part
+                hn[where] = term
+            return carry
+
+        lax.fori_loop(0, TOTAL // CELL, natural, 0, unroll=2)
+        eight = lax.broadcasted_iota(jnp.int32, (8, 128), 0).astype(F32)
+
+        def turned(n, carry):
+            g, s = lax.div(n, 8), lax.rem(n, 8)
+            lanes = pl.ds(pl.multiple_of(8 * g, 8), 8)
+            flow3 = tab_l3[lanes]
+            base4 = tab_l4[lanes]
+            square3 = flow3 * flow3
+            for q in range(6):
+                where = pl.ds((g * 8 + s) * PITCH + 8 * q, 8)
+                flow4 = base4 - slope4 * (eight + (8.0 * q - (N4 / 2 - 0.5)))
+                rest3, rest4 = r_3[where], r_4[where]
+                ht[where] = (square3 - rest3 * rest3) * kk[3] + (
+                    flow4 * flow4 - rest4 * rest4
+                ) * kk[4]
+            return carry
+
+        lax.fori_loop(0, GROUPS * 8, turned, 0)
+
     def from_transposed(dt, coef):
         def take(g, r):
             parts = []
@@ -592,10 +637,6 @@
         def body(n, carry):
             new_line(line_of(n), dt, coef)
 
-            @pl.when(n > 0)
-            def _():
-                start_cols(line_of(n - 1))
-
             @pl.when(n == 3)
             def _():
                 start_low()
@@ -607,7 +648,6 @@
             return carry
 
         lax.fori_loop(0, ROWS_A, body, 0)
-        start_cols(8)
 
     def last_update(dt, coef):
         def move(a, launch):
@@ -660,13 +700,19 @@
         start_cols(other * 6 + a)
         return carry
 
+    def all_cols(a, carry):
+        start_cols(a)
+        return carry
+
+    def own_first(n):
+        return jnp.where(n < 6, half * 6 + n, other * 6 + n - 6)
+
     lax.fori_loop(0, 6, own_cols, 0)
     greet(0)
     early = along_planes(0, 4, zero)
     met_all(0)
     greet(1)
     swaps[0].wait_recv()
-    lax.fori_loop(0, 6, other_cols, 0)
     start_low()
     start_high()
 
@@ -675,43 +721,47 @@
         pack_side()
         start_side()
         if step == 0:
-            swaps[1].start()
+            lax.fori_loop(0, 6, other_cols, 0)
             swaps[2].start()
+            swaps[3].start()
             peak_p = along_planes(4, 9, early)
             met_all(1)
             greet(2)
         else:
+            lax.fori_loop(0, ROWS_A, all_cols, 0)
             peak_p = along_planes(0, 9, zero)
         peak_4 = along_fourth()
         if step == 0:
             met_all(2)
             greet(3)
-        peak_a, peak_b = along_edges()
+        peak_a = along_rows()
         if step == 0:
             met_all(3)
             greet(4)
         wait_side()
         merge_side()
+        peak_3 = along_third()
         if step == 0:
             met_all(4)
             greet(5)
-        peak_3 = along_third()
+        peak_b = along_cols(own_first if step == 0 else lambda n: n)
         if step == 0:
             met_all(5)
         speeds(step, [peak_p, peak_a, peak_b, peak_3, peak_4])
+        gather_terms()
         sent_halos()
         if step == 0:
-            swaps[3].start()
+            swaps[4].start()
             for k in (1, 2):
                 locals_[k].wait()
             bounds(half)
         dt, coef = all_speeds(step)
         from_transposed(dt, coef)
         if step == 0:
-            for k in (1, 2, 3):
+            for k in (1, 2, 3, 4):
                 swaps[k].wait_recv()
             bounds(other)
-            for k in range(4):
+            for k in range(5):
                 swaps[k].wait_send()
         if step < STEPS - 1:
             update(dt, coef)
@@ -740,14 +790,15 @@
         rows(TOTAL), rows(TOTAL), rows(TOTAL), rows(TOTAL), rows(TOTAL), rows(TOTAL),
         rows(TOTAL), rows(TOTAL),
         rows(3 * LINE), rows(3 * LINE), rows(ROWS_A * 72), rows(ROWS_A * 72),
+        rows(TOTAL), rows(TOTAL), rows(TOTAL), rows(trans), rows(trans), rows(24),
         rows(GROUPS * SLOTS * PITCH), rows(trans), rows(trans), rows(trans),
         rows(328), rows(328),
         pltpu.VMEM((TOTAL, 128), jnp.int32), pltpu.VMEM((TOTAL, 128), jnp.int32),
-        rows(24), rows(24), rows(8 * ROWS_A), rows(72), rows(8 * CHUNKS),
+        rows(24), rows(24), rows(8 * ROWS_A), rows(80), rows(8 * CHUNKS),
         rows(8 * GROUPS), rows(8 * GROUPS),
         pltpu.VMEM((STEPS, 1, 128), F32), pltpu.VMEM((STEPS, 128, 1, 128), F32),
         pltpu.SemaphoreType.REGULAR((6,)),
-        dma((3,)), dma((4,)), dma((4,)),
+        dma((3,)), dma((5,)), dma((5,)),
         dma((2,)), dma((2, COLS_B)), dma((2,)), dma((2, ROWS_A)), dma(()), dma(()),
         dma((STEPS,)), dma((STEPS,)),
         dma(()), dma(()), dma(()),

time: 103 us -> 100 us (0.971)
  Pallas kernels: 99.7 us -> 97.3 us
    pallas_call x1, Pallas kernels: 99.7 us -> 97.3 us  [body(): pl.pallas_call(kernel, out_shape=(jax.ShapeDtypeStruct((36, 48, 128), F32...]
where the time goes in v4:
time: 100 us
  Pallas kernels  97.3 us (97%)
  local copies, waits for them, and re-layouts  2.08 us (2%)
    pallas_call x1, Pallas kernels, body(): pl.pallas_call(kernel, out_shape=(jax.ShapeDtypeStruct((36, 48, 128), F32...  97.3 us
    unnamed x6, local copies, waits for them, and re-layouts  2.08 us

profile of v4, /device:TPU:1, one launch (start us, length us, event | category | flops | bytes accessed | tf_op | source)
XLA Modules:
  0.0 100.1 jit_solution(14264031696310419731)
XLA Ops:
  0.6 0.0 copy-start
  0.6 0.0 copy-start.1
  0.7 0.6 copy-done
  1.3 0.0 copy-done.1
  1.3 97.3 %shard_map.68 = (f32[36,48,128]{2,1,0:T(8,128)S(1)}, f32[3]{0:T(128)S(1)}) custom-call(f32[36,48,128]{2,1,0:T(8,128)} %bitcast.29, s32[36,48,128]{2,1,0:T(8,128)} %bitcast.30, s32[36,48,128]{2,1,0:T(8,128)} %bitcast.31, f32[5]{0:T(128)S(1)} %copy-done, f32[5]{0:T(128)S(1)} %copy-done.1), custom_call_target="tpu_custom_call" | custom-call | tf_op jit(solution)/shard_map/pallas_call | solution.py:810
  98.6 0.9 copy.9
  99.6 0.5 copy.10
Async XLA Ops:
  0.6 0.7 copy-start
  0.6 0.7 copy-start.1

commit v5 on v4

--- a/solution.py
+++ b/solution.py
@@ -707,7 +707,6 @@
     def own_first(n):
         return jnp.where(n < 6, half * 6 + n, other * 6 + n - 6)
 
-    lax.fori_loop(0, 6, own_cols, 0)
     greet(0)
     early = along_planes(0, 4, zero)
     met_all(0)
@@ -721,6 +720,7 @@
         pack_side()
         start_side()
         if step == 0:
+            lax.fori_loop(0, 6, own_cols, 0)
             lax.fori_loop(0, 6, other_cols, 0)
             swaps[2].start()
             swaps[3].start()

time: 100 us -> 100 us (level)
  no operation moved by 1% of the time
where the time goes in v5:
time: 100 us
  Pallas kernels  97.3 us (97%)
  local copies, waits for them, and re-layouts  2.08 us (2%)
    pallas_call x1, Pallas kernels, body(): pl.pallas_call(kernel, out_shape=(jax.ShapeDtypeStruct((36, 48, 128), F32...  97.3 us
    unnamed x6, local copies, waits for them, and re-layouts  2.08 us

profile of v5, /device:TPU:1, one launch (start us, length us, event | category | flops | bytes accessed | tf_op | source)
XLA Modules:
  0.0 100.1 jit_solution(1560596359887494805)
XLA Ops:
  0.6 0.0 copy-start
  0.6 0.0 copy-start.1
  0.7 0.6 copy-done
  1.3 0.0 copy-done.1
  1.3 97.3 %shard_map.68 = (f32[36,48,128]{2,1,0:T(8,128)S(1)}, f32[3]{0:T(128)S(1)}) custom-call(f32[36,48,128]{2,1,0:T(8,128)} %bitcast.29, s32[36,48,128]{2,1,0:T(8,128)} %bitcast.30, s32[36,48,128]{2,1,0:T(8,128)} %bitcast.31, f32[5]{0:T(128)S(1)} %copy-done, f32[5]{0:T(128)S(1)} %copy-done.1), custom_call_target="tpu_custom_call" | custom-call | tf_op jit(solution)/shard_map/pallas_call | solution.py:810
  98.6 0.9 copy.9
  99.6 0.5 copy.10
Async XLA Ops:
  0.6 0.7 copy-start
  0.6 0.7 copy-start.1
